TPU v7x, 32 devices: a whole 2x2x4 slice. The times are simulated.
32 devices in a mesh: row: 4 (over x, core), col: 8 (over z, y).
Axes of the slice: x: 2, y: 2, z: 4, core: 2. Of those that a mesh axis runs over, the one named last changes fastest.
Arguments:
- rhs: float32 [4, 8, 8, 4, 128], P('row', 'col'), may hold values from -6 to 6
- diag0: float32 [4, 8, 8, 128], P('row', 'col'), may hold values from 2 to 4
- blocks0: float32 [4, 8, 8, 14, 128, 128], P('row', 'col'), may hold values from -0.1875 to 0.1875
- cols0: int32 [4, 8, 8, 14], P('row', 'col'), may hold values from 0 to 23
- sends0: int32 [4, 8, 4, 4], P('row', 'col'), may hold values from 0 to 7
- pro0: float32 [4, 8, 8, 128, 128], P('row', 'col'), may hold values from -0.5 to 0.5
- agg0: int32 [4, 8, 8], P('row', 'col'), may hold values from 0 to 1
- diag1: float32 [4, 8, 2, 128], P('row', 'col'), may hold values from 2 to 4
- blocks1: float32 [4, 8, 2, 14, 128, 128], P('row', 'col'), may hold values from -0.1875 to 0.1875
- cols1: int32 [4, 8, 2, 14], P('row', 'col'), may hold values from 0 to 9
- sends1: int32 [4, 8, 4, 2], P('row', 'col'), may hold values from 0 to 1
- pro1: float32 [4, 8, 2, 128, 128], P('row', 'col'), may hold values from -0.25 to 0.25
- agg1: int32 [4, 8, 2], P('row', 'col'), may hold values from 0 to 7
- cinv: float32 [1024, 1024], P(('row', 'col')), may hold values from -0.1875 to 0.1875
Outputs:
- solution: float32 [4, 8, 8, 4, 128], P('row', 'col')
Inputs may be any that keep to these rules, and one draw needn't show every extreme that they name: `sends0`: indices of the sender's own fine blocks. `sends1`: indices of the sender's own level-one blocks. `cols0`: indices into the extended fine vector of 24 blocks. `cols1`: indices into the extended level-one vector of 10 blocks. `agg0`: a level-one block of the same partition. `agg1`: a coarsest block, on any partition.
All inputs are finite; a program needn't handle non-finite values.
Results may differ from a plain program's by a relative error of at most 0.0001.
Values sent between devices are 32-bit elements; how exact they have to be, the bound alone decides.
A program may use at most 64 MiB of HBM per device.

v0:
```python
import functools

import jax
import jax.numpy as jnp
from jax import lax
from jax.experimental import pallas as pl
from jax.experimental.pallas import tpu as pltpu
from jax.sharding import PartitionSpec as P

NU = 2
OMEGA = 0.3
F32 = jnp.float32
BF16 = jnp.bfloat16
MESH = pl.DeviceIdType.MESH
NT = (((1,), (1,)), ((), ()))
NN = (((1,), (0,)), ((), ()))


def two_terms(value):
    head = value.astype(BF16)
    tail = (value - head.astype(F32)).astype(BF16)
    return head, tail


def stacked(value):
    head = value.astype(BF16).astype(F32)
    rows = 2 * value.shape[0]
    pad = -rows % 16
    parts = [head, value - head]
    if pad:
        parts.append(jnp.zeros((pad, value.shape[1]), F32))
    return jnp.concatenate(parts, axis=0).astype(BF16)


def product(lhs, head, tail, dims, rows):
    both = lax.dot_general(lhs, head, dims, preferred_element_type=F32) + lax.dot_general(
        lhs, tail, dims, preferred_element_type=F32
    )
    return both[:rows] + both[rows : 2 * rows]


def kernel(
    n_row, n_col,
    cols0_h, sends0_h, agg0_h, cols1_h, sends1_h, agg1_h,
    rhs_h, diag0_h, blocks0_h, pro0_h, diag1_h, blocks1_h, pro1_h, cinv_h,
    out,
    rhs, diag0, blocks0, pro0, diag1, blocks1, pro1, cinv,
    cols0, sends0, agg0, cols1, sends1, agg1,
    in_sem,
    wide0, wide1, phead0, ptail0, phead1, ptail1, chead, ctail,
    dfull0, wfull0, dfull1, wfull1,
    ext0, ext1, x0, x1, b1,
    send0, recv0, send1, recv1,
    aggf, recva, mine, recvc, xs, recvx,
    s_send0, s_recv0, s_send1, s_recv1, s_bsend, s_brecv,
):
    nb, loads, bs = rhs.shape
    nb1 = diag1.shape[0]
    k0 = blocks0.shape[1]
    k1 = blocks1.shape[1]
    g0 = send0.shape[2]
    g1 = send1.shape[2]
    n = n_row * n_col
    owned = cinv.shape[0]
    ncb = cinv.shape[1] // bs
    reps = bs // owned
    row = lax.axis_index("row")
    col = lax.axis_index("col")
    me = row * n_col + col

    def peer(step):
        other = lax.rem(me + step, n)
        return (other // n_col, lax.rem(other, n_col))

    loading = []

    def load(source, target):
        copy = pltpu.make_async_copy(source, target, in_sem.at[len(loading)])
        loading.append(copy)
        copy.start()
        return copy

    l_ints = [
        load(source, target)
        for source, target in (
            (sends0_h, sends0), (cols0_h, cols0), (agg1_h, agg1),
            (agg0_h, agg0), (sends1_h, sends1), (cols1_h, cols1),
        )
    ]
    l_rhs = load(rhs_h, rhs)
    l_diag0 = load(diag0_h, diag0)
    l_blocks0 = [load(blocks0_h.at[b], blocks0.at[b]) for b in range(nb)]
    l_pro0 = load(pro0_h, pro0)
    l_diag1 = load(diag1_h, diag1)
    l_blocks1 = load(blocks1_h, blocks1)
    l_pro1 = load(pro1_h, pro1)
    l_cinv = load(cinv_h, cinv)

    recv0[...] = jnp.zeros_like(recv0)
    recv1[...] = jnp.zeros_like(recv1)

    barrier = pltpu.get_barrier_semaphore()

    def greet(step, carry):
        pl.semaphore_signal(barrier, inc=1, device_id=peer(step), device_id_type=MESH)
        return carry

    lax.fori_loop(1, n, greet, 0)

    directions = (
        (row < n_row - 1, (row + 1, col), row > 0),
        (row > 0, (row - 1, col), row < n_row - 1),
        (col < n_col - 1, (row, col + 1), col > 0),
        (col > 0, (row, col - 1), col < n_col - 1),
    )

    def halo_copy(send, recv, s_send, s_recv, e, d, there):
        return pltpu.make_async_remote_copy(
            src_ref=send.at[e, d], dst_ref=recv.at[e, d],
            send_sem=s_send.at[e, d], recv_sem=s_recv.at[e, d],
            device_id=there, device_id_type=MESH,
        )

    def pack(x, send, sends, e, flip=False):
        for d in range(4):
            for g in range(send.shape[2]):
                send[e, d, g] = x[sends[g, d] if flip else sends[d, g]]

    def start(send, recv, s_send, s_recv, e):
        for d, (goes, there, _) in enumerate(directions):
            @pl.when(goes)
            def _():
                halo_copy(send, recv, s_send, s_recv, e, d, there).start()

    def finish(send, recv, s_send, s_recv, e):
        for d, (_, there, comes) in enumerate(directions):
            @pl.when(comes)
            def _():
                halo_copy(send, recv, s_send, s_recv, e, d, (row, col)).wait_recv()

    def drain(send, recv, s_send, s_recv, e):
        for d, (goes, there, _) in enumerate(directions):
            @pl.when(goes)
            def _():
                halo_copy(send, recv, s_send, s_recv, e, d, there).wait_send()

    level0 = (send0, recv0, s_send0, s_recv0)
    level1 = (send1, recv1, s_send1, s_recv1)

    def own_ext(x, ext, count):
        for b in range(count):
            ext[b] = stacked(x[b])

    def ghost_ext(recv, ext, count, e):
        ghosts = recv.shape[2]
        for d in range(4):
            for g in range(ghosts):
                ext[count + d * ghosts + g] = stacked(recv[e, d, g])

    def coupled(b, cols, ext, wide, k):
        lhs = jnp.concatenate([ext[cols[b, i]] for i in range(k)], axis=1)
        both = lax.dot_general(lhs, wide[b], NN, preferred_element_type=F32)
        both = both[:, :bs] + both[:, bs:]
        return both[:loads] + both[loads : 2 * loads]

    def split_blocks(b, blocks, wide, k):
        def one(i, carry):
            h, t = two_terms(blocks[b, i].T)
            at = pl.ds(pl.multiple_of(i * bs, bs), bs)
            wide[b, at, :bs] = h
            wide[b, at, bs:] = t
            return carry

        lax.fori_loop(0, k, one, 0, unroll=7)

    l_rhs.wait()
    l_diag0.wait()
    for b in range(nb):
        d = jnp.broadcast_to(diag0[b : b + 1, :], (loads, bs))
        w = OMEGA / d
        dfull0[b] = d
        wfull0[b] = w
        x0[b] = w * rhs[b]
    for copy in l_ints:
        copy.wait()
    pack(x0, send0, sends0, 0)
    for b in range(nb1):
        aggf[b : b + 1, :] = jnp.full((1, bs), agg1[b].astype(F32))
    recva[me] = aggf[...]
    pl.semaphore_wait(barrier, n - 1)
    start(*level0, 0)

    def everywhere(src, dst, which):
        def one(there, carry):
            pltpu.make_async_remote_copy(
                src_ref=src, dst_ref=dst.at[me],
                send_sem=s_bsend.at[which], recv_sem=s_brecv.at[which],
                device_id=there, device_id_type=MESH,
            ).start()
            return carry

        half = n_col // 2
        side = col // half

        def far(i, carry):
            across = (1 - side) * half + lax.rem(col + i // n_row, half)
            return one((lax.rem(row + i, n_row), across), carry)

        def near(i, carry):
            beside = side * half + lax.rem(col + i // n_row, half)
            return one((lax.rem(row + i, n_row), beside), carry)

        lax.fori_loop(0, n_row * half, far, 0)
        lax.fori_loop(1, n_row * half, near, 0)

    def all_bytes(dst, sem):
        part = dst.at[pl.ds(0, n - 1)]
        pltpu.make_async_copy(part, part, sem).wait()

    everywhere(aggf, recva, 0)
    own_ext(x0, ext0, nb)
    def arrive(b):
        l_blocks0[b].wait()
        split_blocks(b, blocks0, wide0, k0)

    early = nb
    for b in range(early):
        arrive(b)

    def sweep0(e, into):
        finish(*level0, e)
        ghost_ext(recv0, ext0, nb, e)
        for b in range(nb):
            if e == 0 and b + early < nb:
                arrive(b + early)
            c = coupled(b, cols0, ext0, wide0, k0)
            v = x0[b]
            into[b] = v + wfull0[b] * (rhs[b] - (dfull0[b] * v + c))

    def sweep1(e, right, into):
        finish(*level1, e)
        ghost_ext(recv1, ext1, nb1, e)
        for b in range(nb1):
            c = coupled(b, cols1, ext1, wide1, k1)
            v = x1[b]
            into[b] = v + wfull1[b] * (right[b] - (dfull1[b] * v + c))

    e0 = 0
    for _ in range(NU - 1):
        sweep0(e0, x0)
        e0 += 1
        pack(x0, send0, sends0, e0)
        start(*level0, e0)
        own_ext(x0, ext0, nb)

    l_pro0.wait()
    for b in range(nb):
        h, t = two_terms(pro0[b])
        phead0[b] = h
        ptail0[b] = t
    l_blocks1.wait()
    for b in range(nb1):
        split_blocks(b, blocks1, wide1, k1)
    l_diag1.wait()
    for b in range(nb1):
        d = jnp.broadcast_to(diag1[b : b + 1, :], (loads, bs))
        dfull1[b] = d
        wfull1[b] = OMEGA / d

    finish(*level0, e0)
    ghost_ext(recv0, ext0, nb, e0)
    sums = [jnp.zeros((loads, bs), F32) for _ in range(nb1)]
    for b in range(nb):
        c = coupled(b, cols0, ext0, wide0, k0)
        r = rhs[b] - (dfull0[b] * x0[b] + c)
        q = product(stacked(r), phead0[b], ptail0[b], NN, loads)
        for a in range(nb1):
            sums[a] = sums[a] + jnp.where(agg0[b] == a, q, 0.0)
    e0 += 1

    for b in range(nb1):
        b1[b] = sums[b]
        x1[b] = wfull1[b] * sums[b]
    pack(x1, send1, sends1, 0, True)
    start(*level1, 0)
    own_ext(x1, ext1, nb1)
    l_pro1.wait()
    for b in range(nb1):
        h, t = two_terms(pro1[b])
        phead1[b] = h
        ptail1[b] = t
    l_cinv.wait()
    h, t = two_terms(cinv[...])
    chead[...] = h
    ctail[...] = t
    e1 = 0
    for _ in range(NU - 1):
        sweep1(e1, b1, x1)
        e1 += 1
        pack(x1, send1, sends1, e1, True)
        start(*level1, e1)
        own_ext(x1, ext1, nb1)
    finish(*level1, e1)
    ghost_ext(recv1, ext1, nb1, e1)
    for b in range(nb1):
        c = coupled(b, cols1, ext1, wide1, k1)
        r = b1[b] - (dfull1[b] * x1[b] + c)
        q = product(stacked(r), phead1[b], ptail1[b], NN, loads)
        mine[b * loads : (b + 1) * loads, :] = q
    e1 += 1

    everywhere(mine, recvc, 1)
    recvc[me] = mine[...]
    all_bytes(recva, s_brecv.at[0])
    all_bytes(recvc, s_brecv.at[1])
    index = lax.broadcasted_iota(jnp.int32, (ncb, nb1 * loads, bs), 0).astype(F32)

    def collect(d, total):
        names = recva[d]
        names = jnp.concatenate(
            [jnp.broadcast_to(names[b : b + 1], (loads, bs)) for b in range(nb1)], axis=0
        )
        return total + jnp.where(names[None] == index, recvc[d][None], 0.0)

    total = lax.fori_loop(
        0, n, collect, jnp.zeros((ncb, nb1 * loads, bs), F32), unroll=4
    )
    pieces = []
    for c in range(ncb):
        piece = total[c, :loads]
        for b in range(1, nb1):
            piece = piece + total[c, b * loads : (b + 1) * loads]
        pieces.append(stacked(piece))
    own = product(jnp.concatenate(pieces, axis=1), chead[...], ctail[...], NT, loads)
    wide = jnp.concatenate([own] * reps, axis=1)
    group = lax.broadcasted_iota(jnp.int32, (loads, bs), 1) // owned
    diagonal = group == lax.broadcasted_iota(jnp.int32, (loads, bs), 0)
    xs[...] = jnp.sum(jnp.where(diagonal, wide, 0.0), axis=0, keepdims=True)
    everywhere(xs, recvx, 2)
    recvx[me] = xs[...]
    all_bytes(recvx, s_brecv.at[2])
    for b in range(nb1):
        first = agg1[b] * reps
        parts = jnp.concatenate([recvx[first + t] for t in range(reps)], axis=0)
        piece = jnp.where(diagonal, parts, 0.0)
        for t in range(1, reps):
            turned = jnp.concatenate(
                [parts[:, bs - t * owned :], parts[:, : bs - t * owned]], axis=1
            )
            turned = jnp.where(diagonal, turned, 0.0)
            piece = piece + jnp.concatenate([turned[t:], turned[:t]], axis=0)
        x1[b] = x1[b] + product(stacked(piece), phead1[b], ptail1[b], NT, loads)

    for _ in range(NU):
        pack(x1, send1, sends1, e1, True)
        start(*level1, e1)
        own_ext(x1, ext1, nb1)
        sweep1(e1, b1, x1)
        e1 += 1

    for b in range(nb1):
        ext1[b] = stacked(x1[b])
    for b in range(nb):
        x0[b] = x0[b] + product(ext1[agg0[b]], phead0[b], ptail0[b], NT, loads)
    for i in range(NU):
        pack(x0, send0, sends0, e0)
        start(*level0, e0)
        own_ext(x0, ext0, nb)
        sweep0(e0, out if i == NU - 1 else x0)
        e0 += 1

    for e in range(e0):
        drain(*level0, e)
    for e in range(e1):
        drain(*level1, e)
    all_bytes(recva, s_bsend.at[0])
    all_bytes(recvc, s_bsend.at[1])
    all_bytes(recvx, s_bsend.at[2])


def on_device(
    rhs, diag0, blocks0, cols0, sends0, pro0, agg0, diag1, blocks1, cols1, sends1, pro1, agg1, cinv
):
    n_row, n_col = lax.axis_size("row"), lax.axis_size("col")
    n = n_row * n_col
    _, _, nb, loads, bs = rhs.shape
    nb1 = diag1.shape[2]
    k0, k1 = cols0.shape[3], cols1.shape[3]
    g0, g1 = sends0.shape[3], sends1.shape[3]
    rounds = 2 * NU
    tall = -(-2 * loads // 16) * 16
    floats = [a[0, 0] for a in (rhs, diag0, blocks0, pro0, diag1, blocks1, pro1)] + [cinv]
    ints = [a[0, 0] for a in (cols0, sends0, agg0, cols1)]
    ints += [sends1[0, 0].T, agg1[0, 0]]
    vm = pltpu.VMEM
    dma = pltpu.SemaphoreType.DMA
    scratch = [vm(a.shape, F32) for a in floats]
    scratch += [pltpu.SMEM(a.shape, jnp.int32) for a in ints]
    scratch += [dma((nb + 7 + len(ints),))]
    scratch += [vm((nb, k0 * bs, 2 * bs), BF16), vm((nb1, k1 * bs, 2 * bs), BF16)]
    scratch += [vm((nb, bs, bs), BF16)] * 2
    scratch += [vm((nb1, bs, bs), BF16)] * 2
    scratch += [vm(cinv.shape, BF16)] * 2
    scratch += [vm((nb, loads, bs), F32)] * 2
    scratch += [vm((nb1, loads, bs), F32)] * 2
    scratch += [vm((nb + 4 * g0, tall, bs), BF16), vm((nb1 + 4 * g1, tall, bs), BF16)]
    scratch += [vm((nb, loads, bs), F32), vm((nb1, loads, bs), F32), vm((nb1, loads, bs), F32)]
    scratch += [vm((rounds, 4, g0, loads, bs), F32)] * 2
    scratch += [vm((rounds, 4, g1, loads, bs), F32)] * 2
    scratch += [vm((nb1, bs), F32), vm((n, nb1, bs), F32)]
    scratch += [vm((nb1 * loads, bs), F32), vm((n, nb1 * loads, bs), F32)]
    scratch += [vm((1, bs), F32), vm((n, 1, bs), F32)]
    scratch += [dma((rounds, 4))] * 4 + [dma((3,))] * 2
    result = pl.pallas_call(
        functools.partial(kernel, n_row, n_col),
        out_shape=jax.ShapeDtypeStruct((nb, loads, bs), F32),
        in_specs=[pl.BlockSpec(memory_space=pl.ANY)] * 14,
        out_specs=pl.BlockSpec(memory_space=pltpu.VMEM),
        scratch_shapes=scratch,
        compiler_params=pltpu.CompilerParams(
            collective_id=0, has_side_effects=True, vmem_limit_bytes=60 * 1024 * 1024
        ),
    )(*ints, *floats)
    return result[None, None]


def solution(mesh):
    return jax.shard_map(
        on_device,
        mesh=mesh,
        in_specs=(
            P("row", "col", None, None, None),
            P("row", "col", None, None),
            P("row", "col", None, None, None, None),
            P("row", "col", None, None),
            P("row", "col", None, None),
            P("row", "col", None, None, None),
            P("row", "col", None),
            P("row", "col", None, None),
            P("row", "col", None, None, None, None),
            P("row", "col", None, None),
            P("row", "col", None, None),
            P("row", "col", None, None, None),
            P("row", "col", None),
            P(("row", "col"), None),
        ),
        out_specs=P("row", "col", None, None, None),
        check_vma=False,
    )
```

profile of v0, /device:TPU:0, one launch (start us, length us, event | category | flops | bytes accessed | tf_op | source)
XLA Modules:
  0.0 52.7 jit_solution(11765957419498978433)
XLA Ops:
  0.0 51.4 %shard_map.136 = f32[8,4,128]{2,1,0:T(4,128)} custom-call(s32[8,14]{1,0:T(8,128)} %bitcast.22, s32[4,4]{1,0:T(4,128)} %bitcast.24, s32[8]{0:T(128)} %bitcast.28, s32[2,14]{1,0:T(2,128)} %bitcast.25, s32[2,4]{1,0:T(2,128)} %bitcast.26, s32[2]{0:T(128)} %bitcast.29, f32[8,4,128]{2,1,0:T(4,128)} %bitcast.21, f32[8,128]{1,0:T(8,128)} %bitcast.23, ...), custom_call_target="tpu_custom_call" | custom-call | tf_op jit(solution)/shard_map/pallas_call | solution.py:414
  51.4 1.3 %copy.16 = f32[1,1,8,4,128]{4,3,2,1,0:T(4,128)} copy(f32[1,1,8,4,128]{4,3,2,1,0:T(4,128)} %bitcast.20) | data formatting | bytes 32768
where the time goes:
time: 53 us; the launch traced here: 52.7 us
  Pallas kernels  51.4 us (97%)
  local copies, waits for them, and re-layouts  1.32 us (2%)
    pallas_call x1, Pallas kernels, on_device(): pl.pallas_call(functools.partial(kernel, n_row, n_col), out_shape=jax.Sha...  51.4 us
    unnamed x1, local copies, waits for them, and re-layouts  1.32 us

commit v1 on v0

v1 whole, which is shorter than its diff:
```python
import functools

import jax
import jax.numpy as jnp
from jax import lax
from jax.experimental import pallas as pl
from jax.experimental.pallas import tpu as pltpu
from jax.sharding import PartitionSpec as P

NU = 2
OMEGA = 0.3
F32 = jnp.float32
BF16 = jnp.bfloat16
MESH = pl.DeviceIdType.MESH
NN = (((1,), (0,)), ((), ()))


def two_terms(value):
    head = value.astype(BF16)
    tail = (value - head.astype(F32)).astype(BF16)
    return head, tail


def stacked(value):
    head = value.astype(BF16).astype(F32)
    rows = 2 * value.shape[0]
    pad = -rows % 16
    parts = [head, value - head]
    if pad:
        parts.append(jnp.zeros((pad, value.shape[1]), F32))
    return jnp.concatenate(parts, axis=0).astype(BF16)


def folded(lhs, wide):
    both = lax.dot_general(lhs, wide, NN, preferred_element_type=F32)
    half = both.shape[1] // 2
    return both[:, :half] + both[:, half:]


def joined(lhs, wide, rows):
    both = folded(lhs, wide)
    return both[:rows] + both[rows : 2 * rows]


def seat_of(group, groups, reps):
    if 2 * group + 1 < groups:
        return group * reps + reps - 1
    if 2 * group + 1 > groups:
        return group * reps
    return group * reps + reps // 2


def kernel(
    n_row, n_col, pair,
    cols0_h, sends0_h, agg0_h, cols1_h, sends1_h, agg1_h,
    rhs_h, diag0_h, blocks0_h, pro0_h, diag1_h, blocks1_h, pro1_h, cinv_h,
    out,
    rhs, diag0, blocks0, pro0, diag1, blocks1, pro1,
    cols0, sends0, agg0, cols1, sends1, agg1,
    in_sem,
    wide0, wide1, down0, up0, down1, up1, cin, wide2,
    dfull0, wfull0, dfull1, wfull1,
    ext0, ext1, x0, x1, b1, res0,
    send0, recv0, send1, recv1, psend, precv,
    aggf, recva, mine, recvc, xs, recvx, tally,
    s_send0, s_recv0, s_send1, s_recv1, s_psend, s_precv,
    s_cin, s_cown, s_csend, s_asend, s_msend, s_xsend, s_brecv,
):
    nb, loads, bs = rhs.shape
    nb1 = diag1.shape[0]
    k0 = blocks0.shape[1]
    k1 = blocks1.shape[1]
    g1 = send1.shape[2]
    n = n_row * n_col
    owned, ncu = cinv_h.shape
    ncb = ncu // bs
    reps = bs // owned
    groups = n_col // reps
    ns = (n_row // pair) * groups
    row = lax.axis_index("row")
    col = lax.axis_index("col")
    me = row * n_col + col

    seats = [seat_of(group, groups, reps) for group in range(groups)]
    solvers = [
        (tier * pair + pair - 1, seats[group])
        for tier in range(n_row // pair) for group in range(groups)
    ]
    my_tier, my_group = row // pair, col // reps
    my_seat = jnp.int32(0)
    for group in range(groups):
        my_seat = jnp.where(my_group == group, seats[group], my_seat)
    solving = (lax.rem(row, pair) == pair - 1) & (col == my_seat)
    my_place = my_tier * groups + my_group
    my_slot = lax.rem(row, pair) * reps + lax.rem(col, reps)

    directions = (
        (row < n_row - 1, (row + 1, col), row > 0),
        (row > 0, (row - 1, col), row < n_row - 1),
        (col < n_col - 1, (row, col + 1), col > 0),
        (col > 0, (row, col - 1), col < n_col - 1),
    )

    def wrapped(i, size):
        return jnp.where(i >= size, i - size, i)

    barrier = pltpu.get_barrier_semaphore()

    def greet(r, c):
        pl.semaphore_signal(barrier, inc=1, device_id=(r, c), device_id_type=MESH)

    loading = []

    def load(source, target):
        copy = pltpu.make_async_copy(source, target, in_sem.at[len(loading)])
        loading.append(copy)
        copy.start()
        return copy

    for i in range(1, n_row):
        greet(wrapped(row + i, n_row), col)
    l_ints = [
        load(source, target)
        for source, target in (
            (sends0_h, sends0), (cols0_h, cols0), (agg1_h, agg1),
            (agg0_h, agg0), (sends1_h, sends1), (cols1_h, cols1),
        )
    ]
    l_rhs = load(rhs_h, rhs)
    l_diag0 = load(diag0_h, diag0)
    l_blocks0 = [load(blocks0_h.at[b], blocks0.at[b]) for b in range(nb)]

    def greet_line(i, carry):
        c = wrapped(col + i, n_col)
        for r in range(n_row):
            greet(r, c)
        return carry

    lax.fori_loop(1, n_col, greet_line, 0, unroll=min(n_col - 1, 7))

    l_pro1 = load(pro1_h, pro1)
    l_pro0 = load(pro0_h, pro0)
    l_diag1 = load(diag1_h, diag1)
    l_blocks1 = load(blocks1_h, blocks1)

    for d, (_, _, comes) in enumerate(directions):
        @pl.when(jnp.logical_not(comes))
        def _():
            for e in range(recv0.shape[0]):
                recv0[e, d] = jnp.zeros(recv0.shape[2:], F32)
            for e in range(recv1.shape[0]):
                recv1[e, d] = jnp.zeros(recv1.shape[2:], F32)
            precv[d] = jnp.zeros(precv.shape[1:], F32)

    def halo_copy(send, recv, s_send, s_recv, e, d, there):
        return pltpu.make_async_remote_copy(
            src_ref=send.at[e, d], dst_ref=recv.at[e, d],
            send_sem=s_send.at[e, d], recv_sem=s_recv.at[e, d],
            device_id=there, device_id_type=MESH,
        )

    def pack(x, send, sends, e, flip=False):
        for d in range(4):
            for g in range(send.shape[2]):
                send[e, d, g] = x[sends[g, d] if flip else sends[d, g]]

    def start(send, recv, s_send, s_recv, e):
        for d in (2, 3, 0, 1):
            goes, there, _ = directions[d]

            @pl.when(goes)
            def _():
                halo_copy(send, recv, s_send, s_recv, e, d, there).start()

    def finish(send, recv, s_send, s_recv, e):
        with jax.named_scope("finish"):
            for d, (_, there, comes) in enumerate(directions):
                @pl.when(comes)
                def _():
                    halo_copy(send, recv, s_send, s_recv, e, d, (row, col)).wait_recv()

    def drain(send, recv, s_send, s_recv, e):
        for d, (goes, there, _) in enumerate(directions):
            @pl.when(goes)
            def _():
                halo_copy(send, recv, s_send, s_recv, e, d, there).wait_send()

    level0 = (send0, recv0, s_send0, s_recv0)
    level1 = (send1, recv1, s_send1, s_recv1)

    def bulk_copy(d, g, there):
        return pltpu.make_async_remote_copy(
            src_ref=psend.at[d, g], dst_ref=precv.at[d, g],
            send_sem=s_psend.at[d, g], recv_sem=s_precv.at[d, g],
            device_id=there, device_id_type=MESH,
        )

    def bulk_start(g):
        for d, (goes, there, _) in enumerate(directions):
            psend[d, g, :bs] = pro1[sends1[g, d]]
            psend[d, g, bs:] = jnp.full((8, bs), agg1[sends1[g, d]].astype(F32))

            @pl.when(goes)
            def _():
                bulk_copy(d, g, there).start()

    def own_ext(x, ext, count):
        for b in range(count):
            ext[b] = stacked(x[b])

    def ghost_ext(recv, ext, count, e):
        ghosts = recv.shape[2]
        for d in range(4):
            for g in range(ghosts):
                ext[count + d * ghosts + g] = stacked(recv[e, d, g])

    def coupled(b, cols, ext, wide, k):
        lhs = jnp.concatenate([ext[cols[b, i]] for i in range(k)], axis=1)
        return joined(lhs, wide[b], loads)

    def split_blocks(b, blocks, wide, k):
        def one(i, carry):
            h, t = two_terms(blocks[b, i].T)
            at = pl.ds(pl.multiple_of(i * bs, bs), bs)
            wide[b, at, :bs] = h
            wide[b, at, bs:] = t
            return carry

        lax.fori_loop(0, k, one, 0, unroll=7)

    def arrive(b):
        l_blocks0[b].wait()
        split_blocks(b, blocks0, wide0, k0)

    l_rhs.wait()
    l_diag0.wait()
    for b in range(nb):
        d = jnp.broadcast_to(diag0[b : b + 1, :], (loads, bs))
        w = OMEGA / d
        dfull0[b] = d
        wfull0[b] = w
        x0[b] = w * rhs[b]
    for copy in l_ints:
        copy.wait()
    pack(x0, send0, sends0, 0)
    for b in range(nb1):
        aggf[b * loads : (b + 1) * loads, :] = jnp.full((loads, bs), agg1[b].astype(F32))
    arrive(0)
    with jax.named_scope("barrier"):
        pl.semaphore_wait(barrier, n - 1)
    start(*level0, 0)

    def to_solvers(src, dst, s_send, which, wait=False):
        for i, (r, c) in enumerate(solvers):
            @pl.when((row != r) | (col != c))
            def _():
                copy = pltpu.make_async_remote_copy(
                    src_ref=src, dst_ref=dst.at[me],
                    send_sem=s_send.at[i], recv_sem=s_brecv.at[which],
                    device_id=(r, c), device_id_type=MESH,
                )
                if wait:
                    copy.wait_send()
                else:
                    copy.start()

    def all_bytes(dst, count, sem):
        part = dst.at[pl.ds(0, count)]
        pltpu.make_async_copy(part, part, sem).wait()

    def seat_copy(slot):
        return pltpu.make_async_remote_copy(
            src_ref=cinv_h, dst_ref=cin.at[slot],
            send_sem=s_csend.at[0], recv_sem=s_cin.at[slot],
            device_id=(my_tier * pair + pair - 1, my_seat), device_id_type=MESH,
        )

    own_rows = pltpu.make_async_copy(cinv_h, cin.at[my_slot], s_cown.at[0])

    @pl.when(solving)
    def _():
        own_rows.start()
        recva[me] = aggf[...]

    @pl.when(jnp.logical_not(solving))
    def _():
        seat_copy(my_slot).start()

    to_solvers(aggf, recva, s_asend, 0)
    own_ext(x0, ext0, nb)
    for b in range(1, nb):
        arrive(b)

    def sweep0(e, into):
        finish(*level0, e)
        with jax.named_scope("sweep0"):
            ghost_ext(recv0, ext0, nb, e)
            for b in range(nb):
                c = coupled(b, cols0, ext0, wide0, k0)
                v = x0[b]
                into[b] = v + wfull0[b] * (rhs[b] - (dfull0[b] * v + c))

    def sweep1(right, into):
        with jax.named_scope("sweep1"):
            for b in range(nb1):
                c = coupled(b, cols1, ext1, wide1, k1)
                v = x1[b]
                into[b] = v + wfull1[b] * (right[b] - (dfull1[b] * v + c))

    e0 = 0
    for _ in range(NU - 1):
        sweep0(e0, x0)
        e0 += 1
        pack(x0, send0, sends0, e0)
        start(*level0, e0)
        own_ext(x0, ext0, nb)

    l_pro1.wait()
    bulk_start(0)
    l_pro0.wait()
    for b in range(nb):
        h, t = two_terms(pro0[b])
        down0[b * bs : (b + 1) * bs, :bs] = h
        down0[b * bs : (b + 1) * bs, bs:] = t
    l_blocks1.wait()
    for b in range(nb1):
        split_blocks(b, blocks1, wide1, k1)
    l_diag1.wait()
    for b in range(nb1):
        d = jnp.broadcast_to(diag1[b : b + 1, :], (loads, bs))
        dfull1[b] = d
        wfull1[b] = OMEGA / d

    finish(*level0, e0)
    with jax.named_scope("resid0"):
        ghost_ext(recv0, ext0, nb, e0)
        for b in range(nb):
            c = coupled(b, cols0, ext0, wide0, k0)
            r = rhs[b] - (dfull0[b] * x0[b] + c)
            parts = [jnp.where(agg0[b] == a, r, 0.0) for a in range(nb1)]
            res0[:, b * bs : (b + 1) * bs] = stacked(jnp.concatenate(parts, axis=0))
        q = folded(res0[...], down0[...])
    e0 += 1

    for b in range(nb1):
        low = b * loads
        high = (nb1 + b) * loads
        total = q[low : low + loads] + q[high : high + loads]
        b1[b] = total
        x1[b] = wfull1[b] * total
    pack(x1, send1, sends1, 0, True)
    start(*level1, 0)
    own_ext(x1, ext1, nb1)
    for g in range(1, g1):
        bulk_start(g)
    for b in range(nb1):
        h, t = two_terms(pro1[b])
        down1[b, :, :bs] = h
        down1[b, :, bs:] = t
        h, t = two_terms(pro1[b].T)
        up1[b, :, :bs] = h
        up1[b, :, bs:] = t
    for b in range(nb):
        h, t = two_terms(pro0[b].T)
        up0[b, :, :bs] = h
        up0[b, :, bs:] = t
    e1 = 0
    for _ in range(NU - 1):
        finish(*level1, e1)
        ghost_ext(recv1, ext1, nb1, e1)
        sweep1(b1, x1)
        e1 += 1
        pack(x1, send1, sends1, e1, True)
        start(*level1, e1)
        own_ext(x1, ext1, nb1)

    @pl.when(solving)
    def _():
        own_rows.wait()
        for slot in range(pair * reps):
            @pl.when(my_slot != slot)
            def _():
                seat_copy(slot).wait_recv()

        def one(c, carry):
            at = pl.ds(pl.multiple_of(c * bs, bs), bs)
            for m in range(pair):
                piece = cin[m * reps : (m + 1) * reps, :, at].reshape(bs, bs)
                h, t = two_terms(piece.T)
                wide2[at, m * bs : (m + 1) * bs] = h
                wide2[at, (pair + m) * bs : (pair + m + 1) * bs] = t
            return carry

        lax.fori_loop(0, ncb, one, 0, unroll=4)

    finish(*level1, e1)
    with jax.named_scope("resid1"):
        ghost_ext(recv1, ext1, nb1, e1)
        for b in range(nb1):
            c = coupled(b, cols1, ext1, wide1, k1)
            r = b1[b] - (dfull1[b] * x1[b] + c)
            mine[b * loads : (b + 1) * loads, :] = joined(stacked(r), down1[b], loads)

    to_solvers(mine, recvc, s_msend, 1)

    @pl.when(solving)
    def _():
        recvc[me] = mine[...]

    for d, (_, _, comes) in enumerate(directions):
        for g in range(g1):
            @pl.when(comes)
            def _():
                bulk_copy(d, g, (row, col)).wait_recv()

            h, t = two_terms(precv[d, g, :bs].T)
            up1[nb1 + d * g1 + g, :, :bs] = h
            up1[nb1 + d * g1 + g, :, bs:] = t

    @pl.when(solving)
    def _():
        with jax.named_scope("waitC1"):
            all_bytes(recva, n - 1, s_brecv.at[0])
            all_bytes(recvc, n - 1, s_brecv.at[1])
        index = lax.broadcasted_iota(jnp.int32, (ncb, nb1 * loads, bs), 0).astype(F32)

        def collect(d, total):
            return total + jnp.where(recva[d][None] == index, recvc[d][None], 0.0)

        total = lax.fori_loop(
            0, n, collect, jnp.zeros((ncb, nb1 * loads, bs), F32), unroll=8
        )
        lhs = jnp.concatenate([stacked(total[c]) for c in range(ncb)], axis=1)
        own = folded(lhs, wide2[...])
        rows = [own[i * loads : (i + 1) * loads] for i in range(2 * nb1)]
        own = functools.reduce(lambda a, b: a + b, rows)
        for m in range(pair):
            xs[m] = own[:, m * bs : (m + 1) * bs]

        def tell(r, c):
            pltpu.make_async_remote_copy(
                src_ref=xs, dst_ref=recvx.at[my_place],
                send_sem=s_xsend.at[0], recv_sem=s_brecv.at[2],
                device_id=(r, c), device_id_type=MESH,
            ).start()

        half = n_col // 2
        for i in range(1, n_col):
            step = half + (i // 2 if i % 2 else -(i // 2))
            c = wrapped(col + step, n_col)
            for j in range(n_row):
                tell(wrapped(row + (j + 1) % n_row, n_row), c)
        for j in range(1, n_row):
            tell(wrapped(row + j, n_row), col)
        recvx[my_place] = xs[...]
        with jax.named_scope("waitC2"):
            if ns > 1:
                all_bytes(recvx, ns - 1, s_brecv.at[2])

    @pl.when(jnp.logical_not(solving))
    def _():
        with jax.named_scope("waitC2"):
            all_bytes(recvx, ns, s_brecv.at[2])

    names = [aggf[b * loads : (b + 1) * loads] for b in range(nb1)]
    names += [precv[d, g, bs : bs + loads] for d in range(4) for g in range(g1)]
    names = jnp.stack(names)

    def pick(tier, pieces):
        for m in range(pair):
            for group in range(groups):
                at = ((tier * pair + m) * groups + group).astype(F32)
                block = recvx[tier * groups + group, m]
                pieces = pieces + jnp.where(names == at, block[None], 0.0)
        return pieces

    pieces = lax.fori_loop(0, n_row // pair, pick, jnp.zeros(names.shape, F32), unroll=2)
    for b in range(nb1):
        x1[b] = x1[b] + joined(stacked(pieces[b]), up1[b], loads)
    for d in range(4):
        for g in range(g1):
            v = nb1 + d * g1 + g
            ghost = recv1[e1, d, g] + joined(stacked(pieces[v]), up1[v], loads)
            ext1[v] = stacked(ghost)
    e1 += 1

    for i in range(NU):
        own_ext(x1, ext1, nb1)
        if i > 0:
            finish(*level1, e1)
            ghost_ext(recv1, ext1, nb1, e1)
            e1 += 1
        sweep1(b1, x1)
        if i < NU - 1:
            pack(x1, send1, sends1, e1, True)
            start(*level1, e1)

    own_ext(x1, ext1, nb1)
    for b in range(nb):
        x0[b] = x0[b] + joined(ext1[agg0[b]], up0[b], loads)
    for i in range(NU):
        pack(x0, send0, sends0, e0)
        start(*level0, e0)
        own_ext(x0, ext0, nb)
        sweep0(e0, out if i == NU - 1 else x0)
        e0 += 1

    for e in range(e0):
        drain(*level0, e)
    for e in range(e1):
        drain(*level1, e)
    for d, (goes, there, _) in enumerate(directions):
        for g in range(g1):
            @pl.when(goes)
            def _():
                bulk_copy(d, g, there).wait_send()

    @pl.when(jnp.logical_not(solving))
    def _():
        seat_copy(my_slot).wait_send()

    @pl.when(solving)
    def _():
        all_bytes(tally, n - 1, s_xsend.at[0])

    to_solvers(aggf, recva, s_asend, 0, wait=True)
    to_solvers(mine, recvc, s_msend, 1, wait=True)


def on_device(
    rhs, diag0, blocks0, cols0, sends0, pro0, agg0, diag1, blocks1, cols1, sends1, pro1, agg1, cinv
):
    n_row, n_col = lax.axis_size("row"), lax.axis_size("col")
    n = n_row * n_col
    _, _, nb, loads, bs = rhs.shape
    nb1 = diag1.shape[2]
    k0, k1 = cols0.shape[3], cols1.shape[3]
    g0, g1 = sends0.shape[3], sends1.shape[3]
    owned, ncu = cinv.shape
    reps = bs // owned
    pair = 2 if n_row % 2 == 0 else 1
    ns = (n_row // pair) * (n_col // reps)
    tall = -(-2 * loads // 16) * 16
    floats = [a[0, 0] for a in (rhs, diag0, blocks0, pro0, diag1, blocks1, pro1)]
    ints = [a[0, 0] for a in (cols0, sends0, agg0, cols1)]
    ints += [sends1[0, 0].T, agg1[0, 0]]
    vm = pltpu.VMEM
    dma = pltpu.SemaphoreType.DMA
    scratch = [vm(a.shape, F32) for a in floats]
    scratch += [pltpu.SMEM(a.shape, jnp.int32) for a in ints]
    scratch += [dma((nb + 6 + len(ints),))]
    scratch += [vm((nb, k0 * bs, 2 * bs), BF16), vm((nb1, k1 * bs, 2 * bs), BF16)]
    scratch += [vm((nb * bs, 2 * bs), BF16), vm((nb, bs, 2 * bs), BF16)]
    scratch += [vm((nb1, bs, 2 * bs), BF16), vm((nb1 + 4 * g1, bs, 2 * bs), BF16)]
    scratch += [vm((pair * reps, owned, ncu), F32), vm((ncu, 2 * pair * bs), BF16)]
    scratch += [vm((nb, loads, bs), F32)] * 2
    scratch += [vm((nb1, loads, bs), F32)] * 2
    scratch += [vm((nb + 4 * g0, tall, bs), BF16), vm((nb1 + 4 * g1, tall, bs), BF16)]
    scratch += [vm((nb, loads, bs), F32), vm((nb1, loads, bs), F32), vm((nb1, loads, bs), F32)]
    scratch += [vm((-(-2 * nb1 * loads // 16) * 16, nb * bs), BF16)]
    scratch += [vm((2 * NU, 4, g0, loads, bs), F32)] * 2
    scratch += [vm((2 * NU - 1, 4, g1, loads, bs), F32)] * 2
    scratch += [vm((4, g1, bs + 8, bs), F32)] * 2
    scratch += [vm((nb1 * loads, bs), F32), vm((n, nb1 * loads, bs), F32)]
    scratch += [vm((nb1 * loads, bs), F32), vm((n, nb1 * loads, bs), F32)]
    scratch += [vm((pair, loads, bs), F32), vm((ns, pair, loads, bs), F32)]
    scratch += [vm((n - 1, pair, loads, bs), F32)]
    scratch += [dma((2 * NU, 4))] * 2 + [dma((2 * NU - 1, 4))] * 2 + [dma((4, g1))] * 2
    scratch += [dma((pair * reps,)), dma((1,)), dma((1,))]
    scratch += [dma((ns,))] * 2 + [dma((1,)), dma((3,))]
    result = pl.pallas_call(
        functools.partial(kernel, n_row, n_col, pair),
        out_shape=jax.ShapeDtypeStruct((nb, loads, bs), F32),
        in_specs=[pl.BlockSpec(memory_space=pl.ANY)] * 14,
        out_specs=pl.BlockSpec(memory_space=pltpu.VMEM),
        scratch_shapes=scratch,
        compiler_params=pltpu.CompilerParams(
            collective_id=0, has_side_effects=True, vmem_limit_bytes=60 * 1024 * 1024
        ),
    )(*ints, *floats, cinv)
    return result[None, None]


def solution(mesh):
    return jax.shard_map(
        on_device,
        mesh=mesh,
        in_specs=(
            P("row", "col", None, None, None),
            P("row", "col", None, None),
            P("row", "col", None, None, None, None),
            P("row", "col", None, None),
            P("row", "col", None, None),
            P("row", "col", None, None, None),
            P("row", "col", None),
            P("row", "col", None, None),
            P("row", "col", None, None, None, None),
            P("row", "col", None, None),
            P("row", "col", None, None),
            P("row", "col", None, None, None),
            P("row", "col", None),
            P(("row", "col"), None),
        ),
        out_specs=P("row", "col", None, None, None),
        check_vma=False,
    )
```

time: 53 us -> 48.5 us (0.915)
  Pallas kernels: 51.4 us -> 46.9 us
    pallas_call x1, Pallas kernels: 51.4 us -> 46.9 us  [on_device(): pl.pallas_call(functools.partial(kernel, n_row, n_col, pair), out_shape=j...]
where the time goes in v1:
time: 48.5 us; the launch traced here: 48.3 us
  Pallas kernels  46.9 us (97%)
  local copies, waits for them, and re-layouts  1.32 us (3%)
    pallas_call x1, Pallas kernels, on_device(): pl.pallas_call(functools.partial(kernel, n_row, n_col, pair), out_shape=j...  46.9 us
    unnamed x1, local copies, waits for them, and re-layouts  1.32 us

profile of v1, /device:TPU:0, one launch (start us, length us, event | category | flops | bytes accessed | tf_op | source)
XLA Modules:
  0.0 48.3 jit_solution(11247926081607788617)
XLA Ops:
  0.0 46.9 %shard_map.136 = f32[8,4,128]{2,1,0:T(4,128)} custom-call(s32[8,14]{1,0:T(8,128)} %bitcast.22, s32[4,4]{1,0:T(4,128)} %bitcast.24, s32[8]{0:T(128)} %bitcast.28, s32[2,14]{1,0:T(2,128)} %bitcast.25, s32[2,4]{1,0:T(2,128)} %bitcast.26, s32[2]{0:T(128)} %bitcast.29, f32[8,4,128]{2,1,0:T(4,128)} %bitcast.21, f32[8,128]{1,0:T(8,128)} %bitcast.23, ...), custom_call_target="tpu_custom_call" | custom-call | tf_op jit(solution)/shard_map/pallas_call | solution.py:571
  46.9 1.3 %copy.16 = f32[1,1,8,4,128]{4,3,2,1,0:T(4,128)} copy(f32[1,1,8,4,128]{4,3,2,1,0:T(4,128)} %bitcast.20) | data formatting | bytes 32768

commit v2 on v1

--- a/solution.py
+++ b/solution.py
@@ -55,16 +55,16 @@
     cols0_h, sends0_h, agg0_h, cols1_h, sends1_h, agg1_h,
     rhs_h, diag0_h, blocks0_h, pro0_h, diag1_h, blocks1_h, pro1_h, cinv_h,
     out,
-    rhs, diag0, blocks0, pro0, diag1, blocks1, pro1,
+    rhs, diag0, blocks0, pro0, diag1, blocks1, pro1, cinv,
     cols0, sends0, agg0, cols1, sends1, agg1,
     in_sem,
-    wide0, wide1, down0, up0, down1, up1, cin, wide2,
+    wide0, wide1, folded1, down0, up0, down1, up1, cin, wide2,
     dfull0, wfull0, dfull1, wfull1,
     ext0, ext1, x0, x1, b1, res0,
     send0, recv0, send1, recv1, psend, precv,
     aggf, recva, mine, recvc, xs, recvx, tally,
     s_send0, s_recv0, s_send1, s_recv1, s_psend, s_precv,
-    s_cin, s_cown, s_csend, s_asend, s_msend, s_xsend, s_brecv,
+    s_cin, s_csend, s_asend, s_msend, s_xsend, s_brecv,
 ):
     nb, loads, bs = rhs.shape
     nb1 = diag1.shape[0]
@@ -72,7 +72,7 @@
     k1 = blocks1.shape[1]
     g1 = send1.shape[2]
     n = n_row * n_col
-    owned, ncu = cinv_h.shape
+    owned, ncu = cinv.shape
     ncb = ncu // bs
     reps = bs // owned
     groups = n_col // reps
@@ -128,6 +128,7 @@
     ]
     l_rhs = load(rhs_h, rhs)
     l_diag0 = load(diag0_h, diag0)
+    l_cinv = load(cinv_h, cinv)
     l_blocks0 = [load(blocks0_h.at[b], blocks0.at[b]) for b in range(nb)]
 
     def greet_line(i, carry):
@@ -268,24 +269,48 @@
         part = dst.at[pl.ds(0, count)]
         pltpu.make_async_copy(part, part, sem).wait()
 
-    def seat_copy(slot):
+    shares = s_csend.shape[0]
+    width = ncu // shares
+
+    def seat_copy(slot, share):
+        lanes = pl.ds(share * width, width)
         return pltpu.make_async_remote_copy(
-            src_ref=cinv_h, dst_ref=cin.at[slot],
-            send_sem=s_csend.at[0], recv_sem=s_cin.at[slot],
+            src_ref=cinv.at[:, lanes], dst_ref=cin.at[slot, :, lanes],
+            send_sem=s_csend.at[share], recv_sem=s_cin.at[slot, share],
             device_id=(my_tier * pair + pair - 1, my_seat), device_id_type=MESH,
         )
 
-    own_rows = pltpu.make_async_copy(cinv_h, cin.at[my_slot], s_cown.at[0])
+    def seat_start(share):
+        @pl.when(jnp.logical_not(solving))
+        def _():
+            seat_copy(my_slot, share).start()
+
+    def seat_ready(share):
+        for slot in range(pair * reps):
+            @pl.when(my_slot != slot)
+            def _():
+                seat_copy(slot, share).wait_recv()
+
+        def one(c, carry):
+            at = pl.ds(pl.multiple_of(c * bs, bs), bs)
+            for m in range(pair):
+                piece = cin[m * reps : (m + 1) * reps, :, at].reshape(bs, bs)
+                h, t = two_terms(piece.T)
+                wide2[at, m * bs : (m + 1) * bs] = h
+                wide2[at, (pair + m) * bs : (pair + m + 1) * bs] = t
+            return carry
+
+        first = share * (ncb // shares)
+        lax.fori_loop(first, first + ncb // shares, one, 0, unroll=4 if ncb // shares % 4 == 0 else 1)
+
+    l_cinv.wait()
 
     @pl.when(solving)
     def _():
-        own_rows.start()
+        cin[my_slot] = cinv[...]
         recva[me] = aggf[...]
 
-    @pl.when(jnp.logical_not(solving))
-    def _():
-        seat_copy(my_slot).start()
-
+    seat_start(0)
     to_solvers(aggf, recva, s_asend, 0)
     own_ext(x0, ext0, nb)
     for b in range(1, nb):
@@ -351,8 +376,8 @@
     pack(x1, send1, sends1, 0, True)
     start(*level1, 0)
     own_ext(x1, ext1, nb1)
-    for g in range(1, g1):
-        bulk_start(g)
+    for share in range(1, shares):
+        seat_start(share)
     for b in range(nb1):
         h, t = two_terms(pro1[b])
         down1[b, :, :bs] = h
@@ -360,6 +385,17 @@
         h, t = two_terms(pro1[b].T)
         up1[b, :, :bs] = h
         up1[b, :, bs:] = t
+    for b in range(nb1):
+        twice = jnp.concatenate([down1[b], down1[b]], axis=0)
+
+        def fold(i, carry):
+            at = pl.ds(pl.multiple_of(i * bs, bs), bs)
+            h, t = two_terms(folded(wide1[b, at], twice))
+            folded1[b, at, :bs] = h
+            folded1[b, at, bs:] = t
+            return carry
+
+        lax.fori_loop(0, k1, fold, 0, unroll=7)
     for b in range(nb):
         h, t = two_terms(pro0[b].T)
         up0[b, :, :bs] = h
@@ -376,30 +412,17 @@
 
     @pl.when(solving)
     def _():
-        own_rows.wait()
-        for slot in range(pair * reps):
-            @pl.when(my_slot != slot)
-            def _():
-                seat_copy(slot).wait_recv()
-
-        def one(c, carry):
-            at = pl.ds(pl.multiple_of(c * bs, bs), bs)
-            for m in range(pair):
-                piece = cin[m * reps : (m + 1) * reps, :, at].reshape(bs, bs)
-                h, t = two_terms(piece.T)
-                wide2[at, m * bs : (m + 1) * bs] = h
-                wide2[at, (pair + m) * bs : (pair + m + 1) * bs] = t
-            return carry
-
-        lax.fori_loop(0, ncb, one, 0, unroll=4)
-
+        seat_ready(0)
+
+    base = [
+        joined(stacked(b1[b] - dfull1[b] * x1[b]), down1[b], loads) for b in range(nb1)
+    ]
     finish(*level1, e1)
     with jax.named_scope("resid1"):
         ghost_ext(recv1, ext1, nb1, e1)
         for b in range(nb1):
-            c = coupled(b, cols1, ext1, wide1, k1)
-            r = b1[b] - (dfull1[b] * x1[b] + c)
-            mine[b * loads : (b + 1) * loads, :] = joined(stacked(r), down1[b], loads)
+            c = coupled(b, cols1, ext1, folded1, k1)
+            mine[b * loads : (b + 1) * loads, :] = base[b] - c
 
     to_solvers(mine, recvc, s_msend, 1)
 
@@ -407,18 +430,13 @@
     def _():
         recvc[me] = mine[...]
 
-    for d, (_, _, comes) in enumerate(directions):
-        for g in range(g1):
-            @pl.when(comes)
-            def _():
-                bulk_copy(d, g, (row, col)).wait_recv()
-
-            h, t = two_terms(precv[d, g, :bs].T)
-            up1[nb1 + d * g1 + g, :, :bs] = h
-            up1[nb1 + d * g1 + g, :, bs:] = t
+    for g in range(1, g1):
+        bulk_start(g)
 
     @pl.when(solving)
     def _():
+        for share in range(1, shares):
+            seat_ready(share)
         with jax.named_scope("waitC1"):
             all_bytes(recva, n - 1, s_brecv.at[0])
             all_bytes(recvc, n - 1, s_brecv.at[1])
@@ -453,6 +471,19 @@
         for j in range(1, n_row):
             tell(wrapped(row + j, n_row), col)
         recvx[my_place] = xs[...]
+
+    for d, (_, _, comes) in enumerate(directions):
+        for g in range(g1):
+            @pl.when(comes)
+            def _():
+                bulk_copy(d, g, (row, col)).wait_recv()
+
+            h, t = two_terms(precv[d, g, :bs].T)
+            up1[nb1 + d * g1 + g, :, :bs] = h
+            up1[nb1 + d * g1 + g, :, bs:] = t
+
+    @pl.when(solving)
+    def _():
         with jax.named_scope("waitC2"):
             if ns > 1:
                 all_bytes(recvx, ns - 1, s_brecv.at[2])
@@ -502,29 +533,32 @@
         pack(x0, send0, sends0, e0)
         start(*level0, e0)
         own_ext(x0, ext0, nb)
+        if i == NU - 1:
+            for e in range(e0):
+                drain(*level0, e)
+            for e in range(e1):
+                drain(*level1, e)
+            for d, (goes, there, _) in enumerate(directions):
+                for g in range(g1):
+                    @pl.when(goes)
+                    def _():
+                        bulk_copy(d, g, there).wait_send()
+
+            @pl.when(jnp.logical_not(solving))
+            def _():
+                for share in range(shares):
+                    seat_copy(my_slot, share).wait_send()
+
+            @pl.when(solving)
+            def _():
+                all_bytes(tally, n - 1, s_xsend.at[0])
+
+            to_solvers(aggf, recva, s_asend, 0, wait=True)
+            to_solvers(mine, recvc, s_msend, 1, wait=True)
         sweep0(e0, out if i == NU - 1 else x0)
         e0 += 1
 
-    for e in range(e0):
-        drain(*level0, e)
-    for e in range(e1):
-        drain(*level1, e)
-    for d, (goes, there, _) in enumerate(directions):
-        for g in range(g1):
-            @pl.when(goes)
-            def _():
-                bulk_copy(d, g, there).wait_send()
-
-    @pl.when(jnp.logical_not(solving))
-    def _():
-        seat_copy(my_slot).wait_send()
-
-    @pl.when(solving)
-    def _():
-        all_bytes(tally, n - 1, s_xsend.at[0])
-
-    to_solvers(aggf, recva, s_asend, 0, wait=True)
-    to_solvers(mine, recvc, s_msend, 1, wait=True)
+    drain(*level0, e0 - 1)
 
 
 def on_device(
@@ -540,16 +574,17 @@
     reps = bs // owned
     pair = 2 if n_row % 2 == 0 else 1
     ns = (n_row // pair) * (n_col // reps)
+    shares = 2 if (ncu // bs) % 2 == 0 else 1
     tall = -(-2 * loads // 16) * 16
-    floats = [a[0, 0] for a in (rhs, diag0, blocks0, pro0, diag1, blocks1, pro1)]
+    floats = [a[0, 0] for a in (rhs, diag0, blocks0, pro0, diag1, blocks1, pro1)] + [cinv]
     ints = [a[0, 0] for a in (cols0, sends0, agg0, cols1)]
     ints += [sends1[0, 0].T, agg1[0, 0]]
     vm = pltpu.VMEM
     dma = pltpu.SemaphoreType.DMA
     scratch = [vm(a.shape, F32) for a in floats]
     scratch += [pltpu.SMEM(a.shape, jnp.int32) for a in ints]
-    scratch += [dma((nb + 6 + len(ints),))]
-    scratch += [vm((nb, k0 * bs, 2 * bs), BF16), vm((nb1, k1 * bs, 2 * bs), BF16)]
+    scratch += [dma((nb + 7 + len(ints),))]
+    scratch += [vm((nb, k0 * bs, 2 * bs), BF16)] + [vm((nb1, k1 * bs, 2 * bs), BF16)] * 2
     scratch += [vm((nb * bs, 2 * bs), BF16), vm((nb, bs, 2 * bs), BF16)]
     scratch += [vm((nb1, bs, 2 * bs), BF16), vm((nb1 + 4 * g1, bs, 2 * bs), BF16)]
     scratch += [vm((pair * reps, owned, ncu), F32), vm((ncu, 2 * pair * bs), BF16)]
@@ -566,18 +601,18 @@
     scratch += [vm((pair, loads, bs), F32), vm((ns, pair, loads, bs), F32)]
     scratch += [vm((n - 1, pair, loads, bs), F32)]
     scratch += [dma((2 * NU, 4))] * 2 + [dma((2 * NU - 1, 4))] * 2 + [dma((4, g1))] * 2
-    scratch += [dma((pair * reps,)), dma((1,)), dma((1,))]
+    scratch += [dma((pair * reps, shares)), dma((shares,))]
     scratch += [dma((ns,))] * 2 + [dma((1,)), dma((3,))]
     result = pl.pallas_call(
         functools.partial(kernel, n_row, n_col, pair),
-        out_shape=jax.ShapeDtypeStruct((nb, loads, bs), F32),
+        out_shape=pltpu.VMEM((nb, loads, bs), F32),
         in_specs=[pl.BlockSpec(memory_space=pl.ANY)] * 14,
         out_specs=pl.BlockSpec(memory_space=pltpu.VMEM),
         scratch_shapes=scratch,
         compiler_params=pltpu.CompilerParams(
             collective_id=0, has_side_effects=True, vmem_limit_bytes=60 * 1024 * 1024
         ),
-    )(*ints, *floats, cinv)
+    )(*ints, *floats)
     return result[None, None]
 
 

time: 48.5 us -> 44.8 us (0.924)
  Pallas kernels: 46.9 us -> 44 us
  local copies, waits for them, and re-layouts: 1.32 us -> 0.61 us
    pallas_call x1, Pallas kernels: 46.9 us -> 44 us  [on_device(): pl.pallas_call(functools.partial(kernel, n_row, n_col, pair), out_shape=p...]
    unnamed x1, local copies, waits for them, and re-layouts: 1.32 us -> 0.61 us
where the time goes in v2:
time: 44.8 us; the launch traced here: 44.6 us
  Pallas kernels  44 us (98%)
  local copies, waits for them, and re-layouts  0.61 us (1%)
    pallas_call x1, Pallas kernels, on_device(): pl.pallas_call(functools.partial(kernel, n_row, n_col, pair), out_shape=p...  44 us

profile of v2, /device:TPU:0, one launch (start us, length us, event | category | flops | bytes accessed | tf_op | source)
XLA Modules:
  0.0 44.6 jit_solution(2349852568069741026)
XLA Ops:
  0.0 44.0 %shard_map.136 = f32[8,4,128]{2,1,0:T(4,128)S(1)} custom-call(s32[8,14]{1,0:T(8,128)} %bitcast.22, s32[4,4]{1,0:T(4,128)} %bitcast.24, s32[8]{0:T(128)} %bitcast.28, s32[2,14]{1,0:T(2,128)} %bitcast.25, s32[2,4]{1,0:T(2,128)} %bitcast.26, s32[2]{0:T(128)} %bitcast.29, f32[8,4,128]{2,1,0:T(4,128)} %bitcast.21, f32[8,128]{1,0:T(8,128)} %bitcast.23, ...), custom_call_target="tpu_custom_call" | custom-call | tf_op jit(solution)/shard_map/pallas_call | solution.py:606
  44.0 0.6 %copy.16 = f32[1,1,8,4,128]{4,3,2,1,0:T(4,128)} copy(f32[1,1,8,4,128]{4,3,2,1,0:T(4,128)S(1)} %bitcast.16) | data formatting | bytes 32768

commit v3 on v2

--- a/solution.py
+++ b/solution.py
@@ -48,6 +48,34 @@
     if 2 * group + 1 > groups:
         return group * reps
     return group * reps + reps // 2
+
+
+def reaches(n_row, n_col, pair, groups, reps):
+    grid = [(r, c) for r in range(n_row) for c in range(n_col)]
+
+    def beside(p, row_steps, col_steps):
+        steps = [(d, 0) for d in row_steps] + [(0, d) for d in col_steps]
+        spots = [(p[0] + a, p[1] + b) for a, b in steps]
+        return [q for q in spots if 0 <= q[0] < n_row and 0 <= q[1] < n_col]
+
+    def heard(known, jump):
+        told = {}
+        for p in grid:
+            near = beside(p, (-1, 1), (-1, 1)) + (beside(p, (), (-2, 2)) if jump else [])
+            told[p] = known[p].union(*[known[q] for q in near])
+        return told
+
+    first = heard({p: {p} for p in grid}, False)
+    second = heard(first, False)
+    third = heard(second, True)
+    last = heard(heard(third, True), False)
+    seats = [seat_of(group, groups, reps) for group in range(groups)]
+    for r, c in grid:
+        own = (r // pair * pair + pair - 1, seats[c // reps])
+        solvers = {(t, s) for t in range(pair - 1, n_row, pair) for s in seats}
+        if own not in third[(r, c)] or not solvers <= last[(r, c)]:
+            return False
+    return True
 
 
 def kernel(
@@ -63,8 +91,8 @@
     ext0, ext1, x0, x1, b1, res0,
     send0, recv0, send1, recv1, psend, precv,
     aggf, recva, mine, recvc, xs, recvx, tally,
-    s_send0, s_recv0, s_send1, s_recv1, s_psend, s_precv,
-    s_cin, s_csend, s_asend, s_msend, s_xsend, s_brecv,
+    s_send, s_recv, s_psend, s_precv,
+    s_cin, s_csend, s_asend, s_msend, s_xsend, s_brecv, s_far,
 ):
     nb, loads, bs = rhs.shape
     nb1 = diag1.shape[0]
@@ -105,6 +133,7 @@
         return jnp.where(i >= size, i - size, i)
 
     barrier = pltpu.get_barrier_semaphore()
+    relayed = reaches(n_row, n_col, pair, groups, reps)
 
     def greet(r, c):
         pl.semaphore_signal(barrier, inc=1, device_id=(r, c), device_id_type=MESH)
@@ -112,37 +141,40 @@
     loading = []
 
     def load(source, target):
-        copy = pltpu.make_async_copy(source, target, in_sem.at[len(loading)])
+        copy = pltpu.make_async_copy(source, target, in_sem.at[len(loading) % in_sem.shape[0]])
         loading.append(copy)
         copy.start()
         return copy
 
-    for i in range(1, n_row):
-        greet(wrapped(row + i, n_row), col)
+    if relayed:
+        for goes, (r, c), _ in directions:
+            @pl.when(goes)
+            def _():
+                greet(r, c)
+    else:
+        for i in range(1, n_row):
+            greet(wrapped(row + i, n_row), col)
+
     l_ints = [
         load(source, target)
         for source, target in (
-            (sends0_h, sends0), (cols0_h, cols0), (agg1_h, agg1),
-            (agg0_h, agg0), (sends1_h, sends1), (cols1_h, cols1),
+            (sends0_h, sends0), (sends1_h, sends1), (agg1_h, agg1),
+            (agg0_h, agg0), (cols0_h, cols0), (cols1_h, cols1),
         )
     ]
     l_rhs = load(rhs_h, rhs)
     l_diag0 = load(diag0_h, diag0)
-    l_cinv = load(cinv_h, cinv)
+    l_pro1 = load(pro1_h, pro1)
     l_blocks0 = [load(blocks0_h.at[b], blocks0.at[b]) for b in range(nb)]
 
-    def greet_line(i, carry):
-        c = wrapped(col + i, n_col)
-        for r in range(n_row):
-            greet(r, c)
-        return carry
-
-    lax.fori_loop(1, n_col, greet_line, 0, unroll=min(n_col - 1, 7))
-
-    l_pro1 = load(pro1_h, pro1)
-    l_pro0 = load(pro0_h, pro0)
-    l_diag1 = load(diag1_h, diag1)
-    l_blocks1 = load(blocks1_h, blocks1)
+    if not relayed:
+        def greet_line(i, carry):
+            c = wrapped(col + i, n_col)
+            for r in range(n_row):
+                greet(r, c)
+            return carry
+
+        lax.fori_loop(1, n_col, greet_line, 0, unroll=min(n_col - 1, 7))
 
     for d, (_, _, comes) in enumerate(directions):
         @pl.when(jnp.logical_not(comes))
@@ -153,10 +185,14 @@
                 recv1[e, d] = jnp.zeros(recv1.shape[2:], F32)
             precv[d] = jnp.zeros(precv.shape[1:], F32)
 
-    def halo_copy(send, recv, s_send, s_recv, e, d, there):
+    order = []
+
+    def halo_copy(level, e, d, there):
+        send, recv = level
+        turn = order.index((level is level1, e)) % 2
         return pltpu.make_async_remote_copy(
             src_ref=send.at[e, d], dst_ref=recv.at[e, d],
-            send_sem=s_send.at[e, d], recv_sem=s_recv.at[e, d],
+            send_sem=s_send.at[turn, d], recv_sem=s_recv.at[turn, d],
             device_id=there, device_id_type=MESH,
         )
 
@@ -165,29 +201,33 @@
             for g in range(send.shape[2]):
                 send[e, d, g] = x[sends[g, d] if flip else sends[d, g]]
 
-    def start(send, recv, s_send, s_recv, e):
+    def start(level, e):
+        order.append((level is level1, e))
         for d in (2, 3, 0, 1):
             goes, there, _ = directions[d]
 
             @pl.when(goes)
             def _():
-                halo_copy(send, recv, s_send, s_recv, e, d, there).start()
-
-    def finish(send, recv, s_send, s_recv, e):
+                halo_copy(level, e, d, there).start()
+
+    def finish(level, e):
         with jax.named_scope("finish"):
             for d, (_, there, comes) in enumerate(directions):
                 @pl.when(comes)
                 def _():
-                    halo_copy(send, recv, s_send, s_recv, e, d, (row, col)).wait_recv()
-
-    def drain(send, recv, s_send, s_recv, e):
+                    halo_copy(level, e, d, (row, col)).wait_recv()
+
+    def drain(back):
+        if back > len(order):
+            return
+        upper, e = order[-back]
         for d, (goes, there, _) in enumerate(directions):
             @pl.when(goes)
             def _():
-                halo_copy(send, recv, s_send, s_recv, e, d, there).wait_send()
-
-    level0 = (send0, recv0, s_send0, s_recv0)
-    level1 = (send1, recv1, s_send1, s_recv1)
+                halo_copy(level1 if upper else level0, e, d, there).wait_send()
+
+    level0 = (send0, recv0)
+    level1 = (send1, recv1)
 
     def bulk_copy(d, g, there):
         return pltpu.make_async_remote_copy(
@@ -244,26 +284,50 @@
     for copy in l_ints:
         copy.wait()
     pack(x0, send0, sends0, 0)
+    with jax.named_scope("barrier"):
+        if relayed:
+            count = jnp.int32(0)
+            for _, _, comes in directions:
+                count = count + jnp.where(comes, 1, 0)
+            pl.semaphore_wait(barrier, count)
+        else:
+            pl.semaphore_wait(barrier, n - 1)
+    start(level0, 0)
+    l_pro1.wait()
+    bulk_start(0)
+    l_cinv = load(cinv_h, cinv)
+    l_pro0 = load(pro0_h, pro0)
+    l_diag1 = load(diag1_h, diag1)
+    l_blocks1 = load(blocks1_h, blocks1)
+    own_ext(x0, ext0, nb)
     for b in range(nb1):
-        aggf[b * loads : (b + 1) * loads, :] = jnp.full((loads, bs), agg1[b].astype(F32))
-    arrive(0)
-    with jax.named_scope("barrier"):
-        pl.semaphore_wait(barrier, n - 1)
-    start(*level0, 0)
-
-    def to_solvers(src, dst, s_send, which, wait=False):
-        for i, (r, c) in enumerate(solvers):
+        aggf[b : b + 1, :] = jnp.full((1, bs), agg1[b].astype(F32))
+    for b in range(nb):
+        arrive(b)
+
+    def tell_far(jump):
+        if relayed:
+            for goes, c in ((col + 2 < n_col, col + 2), (col > 1, col - 2)):
+                @pl.when(goes)
+                def _():
+                    pl.semaphore_signal(
+                        s_far.at[jump], inc=1, device_id=(row, c), device_id_type=MESH
+                    )
+
+    def hear_far(jump):
+        if relayed:
+            count = jnp.where(col + 2 < n_col, 1, 0) + jnp.where(col > 1, 1, 0)
+            pl.semaphore_wait(s_far.at[jump], count)
+
+    def to_solvers(src, dst, s_out, which):
+        for r, c in solvers:
             @pl.when((row != r) | (col != c))
             def _():
-                copy = pltpu.make_async_remote_copy(
+                pltpu.make_async_remote_copy(
                     src_ref=src, dst_ref=dst.at[me],
-                    send_sem=s_send.at[i], recv_sem=s_brecv.at[which],
+                    send_sem=s_out.at[0], recv_sem=s_brecv.at[which],
                     device_id=(r, c), device_id_type=MESH,
-                )
-                if wait:
-                    copy.wait_send()
-                else:
-                    copy.start()
+                ).start()
 
     def all_bytes(dst, count, sem):
         part = dst.at[pl.ds(0, count)]
@@ -276,7 +340,7 @@
         lanes = pl.ds(share * width, width)
         return pltpu.make_async_remote_copy(
             src_ref=cinv.at[:, lanes], dst_ref=cin.at[slot, :, lanes],
-            send_sem=s_csend.at[share], recv_sem=s_cin.at[slot, share],
+            send_sem=s_csend.at[share], recv_sem=s_cin.at[share],
             device_id=(my_tier * pair + pair - 1, my_seat), device_id_type=MESH,
         )
 
@@ -286,10 +350,9 @@
             seat_copy(my_slot, share).start()
 
     def seat_ready(share):
-        for slot in range(pair * reps):
-            @pl.when(my_slot != slot)
-            def _():
-                seat_copy(slot, share).wait_recv()
+        if pair * reps > 1:
+            part = cin.at[pl.ds(0, pair * reps - 1), :, pl.ds(share * width, width)]
+            pltpu.make_async_copy(part, part, s_cin.at[share]).wait()
 
         def one(c, carry):
             at = pl.ds(pl.multiple_of(c * bs, bs), bs)
@@ -303,21 +366,10 @@
         first = share * (ncb // shares)
         lax.fori_loop(first, first + ncb // shares, one, 0, unroll=4 if ncb // shares % 4 == 0 else 1)
 
-    l_cinv.wait()
-
-    @pl.when(solving)
-    def _():
-        cin[my_slot] = cinv[...]
-        recva[me] = aggf[...]
-
-    seat_start(0)
-    to_solvers(aggf, recva, s_asend, 0)
-    own_ext(x0, ext0, nb)
-    for b in range(1, nb):
-        arrive(b)
-
     def sweep0(e, into):
-        finish(*level0, e)
+        finish(level0, e)
+        if e == 0:
+            tell_far(0)
         with jax.named_scope("sweep0"):
             ghost_ext(recv0, ext0, nb, e)
             for b in range(nb):
@@ -337,11 +389,19 @@
         sweep0(e0, x0)
         e0 += 1
         pack(x0, send0, sends0, e0)
-        start(*level0, e0)
+        start(level0, e0)
         own_ext(x0, ext0, nb)
 
-    l_pro1.wait()
-    bulk_start(0)
+    for g in range(1, g1):
+        bulk_start(g)
+    drain(2)
+    l_cinv.wait()
+
+    @pl.when(solving)
+    def _():
+        cin[my_slot] = cinv[...]
+        recva[me] = aggf[...]
+
     l_pro0.wait()
     for b in range(nb):
         h, t = two_terms(pro0[b])
@@ -356,7 +416,9 @@
         dfull1[b] = d
         wfull1[b] = OMEGA / d
 
-    finish(*level0, e0)
+    finish(level0, e0)
+    hear_far(0)
+    tell_far(1)
     with jax.named_scope("resid0"):
         ghost_ext(recv0, ext0, nb, e0)
         for b in range(nb):
@@ -374,10 +436,10 @@
         b1[b] = total
         x1[b] = wfull1[b] * total
     pack(x1, send1, sends1, 0, True)
-    start(*level1, 0)
+    start(level1, 0)
     own_ext(x1, ext1, nb1)
-    for share in range(1, shares):
-        seat_start(share)
+    seat_start(0)
+    drain(2)
     for b in range(nb1):
         h, t = two_terms(pro1[b])
         down1[b, :, :bs] = h
@@ -402,13 +464,19 @@
         up0[b, :, bs:] = t
     e1 = 0
     for _ in range(NU - 1):
-        finish(*level1, e1)
+        finish(level1, e1)
+        if e1 == 0:
+            hear_far(1)
         ghost_ext(recv1, ext1, nb1, e1)
         sweep1(b1, x1)
         e1 += 1
         pack(x1, send1, sends1, e1, True)
-        start(*level1, e1)
+        start(level1, e1)
+        drain(2)
         own_ext(x1, ext1, nb1)
+
+    for share in range(1, shares):
+        seat_start(share)
 
     @pl.when(solving)
     def _():
@@ -417,7 +485,8 @@
     base = [
         joined(stacked(b1[b] - dfull1[b] * x1[b]), down1[b], loads) for b in range(nb1)
     ]
-    finish(*level1, e1)
+    finish(level1, e1)
+    to_solvers(aggf, recva, s_asend, 0)
     with jax.named_scope("resid1"):
         ghost_ext(recv1, ext1, nb1, e1)
         for b in range(nb1):
@@ -429,9 +498,6 @@
     @pl.when(solving)
     def _():
         recvc[me] = mine[...]
-
-    for g in range(1, g1):
-        bulk_start(g)
 
     @pl.when(solving)
     def _():
@@ -443,7 +509,11 @@
         index = lax.broadcasted_iota(jnp.int32, (ncb, nb1 * loads, bs), 0).astype(F32)
 
         def collect(d, total):
-            return total + jnp.where(recva[d][None] == index, recvc[d][None], 0.0)
+            name = recva[d]
+            name = jnp.concatenate(
+                [jnp.broadcast_to(name[b : b + 1], (loads, bs)) for b in range(nb1)], axis=0
+            )
+            return total + jnp.where(name[None] == index, recvc[d][None], 0.0)
 
         total = lax.fori_loop(
             0, n, collect, jnp.zeros((ncb, nb1 * loads, bs), F32), unroll=8
@@ -493,7 +563,7 @@
         with jax.named_scope("waitC2"):
             all_bytes(recvx, ns, s_brecv.at[2])
 
-    names = [aggf[b * loads : (b + 1) * loads] for b in range(nb1)]
+    names = [jnp.broadcast_to(aggf[b : b + 1], (loads, bs)) for b in range(nb1)]
     names += [precv[d, g, bs : bs + loads] for d in range(4) for g in range(g1)]
     names = jnp.stack(names)
 
@@ -518,26 +588,24 @@
     for i in range(NU):
         own_ext(x1, ext1, nb1)
         if i > 0:
-            finish(*level1, e1)
+            finish(level1, e1)
             ghost_ext(recv1, ext1, nb1, e1)
             e1 += 1
         sweep1(b1, x1)
         if i < NU - 1:
             pack(x1, send1, sends1, e1, True)
-            start(*level1, e1)
+            start(level1, e1)
+            drain(2)
 
     own_ext(x1, ext1, nb1)
     for b in range(nb):
         x0[b] = x0[b] + joined(ext1[agg0[b]], up0[b], loads)
     for i in range(NU):
         pack(x0, send0, sends0, e0)
-        start(*level0, e0)
+        start(level0, e0)
         own_ext(x0, ext0, nb)
+        drain(2)
         if i == NU - 1:
-            for e in range(e0):
-                drain(*level0, e)
-            for e in range(e1):
-                drain(*level1, e)
             for d, (goes, there, _) in enumerate(directions):
                 for g in range(g1):
                     @pl.when(goes)
@@ -548,17 +616,20 @@
             def _():
                 for share in range(shares):
                     seat_copy(my_slot, share).wait_send()
+                all_bytes(recva, ns, s_asend.at[0])
+                all_bytes(recvc, ns, s_msend.at[0])
 
             @pl.when(solving)
             def _():
                 all_bytes(tally, n - 1, s_xsend.at[0])
-
-            to_solvers(aggf, recva, s_asend, 0, wait=True)
-            to_solvers(mine, recvc, s_msend, 1, wait=True)
+                if ns > 1:
+                    all_bytes(recva, ns - 1, s_asend.at[0])
+                    all_bytes(recvc, ns - 1, s_msend.at[0])
+
         sweep0(e0, out if i == NU - 1 else x0)
         e0 += 1
 
-    drain(*level0, e0 - 1)
+    drain(1)
 
 
 def on_device(
@@ -583,7 +654,7 @@
     dma = pltpu.SemaphoreType.DMA
     scratch = [vm(a.shape, F32) for a in floats]
     scratch += [pltpu.SMEM(a.shape, jnp.int32) for a in ints]
-    scratch += [dma((nb + 7 + len(ints),))]
+    scratch += [dma((nb + 3 + len(ints),))]
     scratch += [vm((nb, k0 * bs, 2 * bs), BF16)] + [vm((nb1, k1 * bs, 2 * bs), BF16)] * 2
     scratch += [vm((nb * bs, 2 * bs), BF16), vm((nb, bs, 2 * bs), BF16)]
     scratch += [vm((nb1, bs, 2 * bs), BF16), vm((nb1 + 4 * g1, bs, 2 * bs), BF16)]
@@ -596,13 +667,13 @@
     scratch += [vm((2 * NU, 4, g0, loads, bs), F32)] * 2
     scratch += [vm((2 * NU - 1, 4, g1, loads, bs), F32)] * 2
     scratch += [vm((4, g1, bs + 8, bs), F32)] * 2
-    scratch += [vm((nb1 * loads, bs), F32), vm((n, nb1 * loads, bs), F32)]
+    scratch += [vm((nb1, bs), F32), vm((n, nb1, bs), F32)]
     scratch += [vm((nb1 * loads, bs), F32), vm((n, nb1 * loads, bs), F32)]
     scratch += [vm((pair, loads, bs), F32), vm((ns, pair, loads, bs), F32)]
     scratch += [vm((n - 1, pair, loads, bs), F32)]
-    scratch += [dma((2 * NU, 4))] * 2 + [dma((2 * NU - 1, 4))] * 2 + [dma((4, g1))] * 2
-    scratch += [dma((pair * reps, shares)), dma((shares,))]
-    scratch += [dma((ns,))] * 2 + [dma((1,)), dma((3,))]
+    scratch += [dma((2, 4))] * 2 + [dma((4, g1))] * 2
+    scratch += [dma((shares,))] * 2 + [dma((1,))] * 3 + [dma((3,))]
+    scratch += [pltpu.SemaphoreType.REGULAR((2,))]
     result = pl.pallas_call(
         functools.partial(kernel, n_row, n_col, pair),
         out_shape=pltpu.VMEM((nb, loads, bs), F32),

time: 44.8 us -> 42.1 us (0.940)
  Pallas kernels: 44 us -> 41.3 us
    pallas_call x1, Pallas kernels: 44 us -> 41.3 us  [on_device(): pl.pallas_call(functools.partial(kernel, n_row, n_col, pair), out_shape=p...]
where the time goes in v3:
time: 42.1 us; the launch traced here: 42 us
  Pallas kernels  41.3 us (98%)
  local copies, waits for them, and re-layouts  0.61 us (1%)
    pallas_call x1, Pallas kernels, on_device(): pl.pallas_call(functools.partial(kernel, n_row, n_col, pair), out_shape=p...  41.3 us

profile of v3, /device:TPU:0, one launch (start us, length us, event | category | flops | bytes accessed | tf_op | source)
XLA Modules:
  0.0 42.0 jit_solution(11752475502491144886)
XLA Ops:
  0.0 41.3 %shard_map.136 = f32[8,4,128]{2,1,0:T(4,128)S(1)} custom-call(s32[8,14]{1,0:T(8,128)} %bitcast.22, s32[4,4]{1,0:T(4,128)} %bitcast.24, s32[8]{0:T(128)} %bitcast.28, s32[2,14]{1,0:T(2,128)} %bitcast.25, s32[2,4]{1,0:T(2,128)} %bitcast.26, s32[2]{0:T(128)} %bitcast.29, f32[8,4,128]{2,1,0:T(4,128)} %bitcast.21, f32[8,128]{1,0:T(8,128)} %bitcast.23, ...), custom_call_target="tpu_custom_call" | custom-call | tf_op jit(solution)/shard_map/pallas_call | solution.py:677
  41.3 0.6 %copy.16 = f32[1,1,8,4,128]{4,3,2,1,0:T(4,128)} copy(f32[1,1,8,4,128]{4,3,2,1,0:T(4,128)S(1)} %bitcast.16) | data formatting | bytes 32768

commit v4 on v3

--- a/solution.py
+++ b/solution.py
@@ -67,13 +67,17 @@
 
     first = heard({p: {p} for p in grid}, False)
     second = heard(first, False)
+    early = {}
+    for r, c in grid:
+        far = [(r, c + d) for d in (-2, 2) if 0 <= c + d < n_col]
+        early[(r, c)] = second[(r, c)].union(*[second[q] for q in far])
     third = heard(second, True)
     last = heard(heard(third, True), False)
     seats = [seat_of(group, groups, reps) for group in range(groups)]
     for r, c in grid:
+        solvers = {(t, s) for t in range(pair - 1, n_row, pair) for s in seats}
         own = (r // pair * pair + pair - 1, seats[c // reps])
-        solvers = {(t, s) for t in range(pair - 1, n_row, pair) for s in seats}
-        if own not in third[(r, c)] or not solvers <= last[(r, c)]:
+        if own not in early[(r, c)] or not solvers <= last[(r, c)]:
             return False
     return True
 
@@ -147,7 +151,7 @@
         return copy
 
     if relayed:
-        for goes, (r, c), _ in directions:
+        for goes, (r, c) in [(goes, there) for goes, there, _ in directions]:
             @pl.when(goes)
             def _():
                 greet(r, c)
@@ -155,17 +159,14 @@
         for i in range(1, n_row):
             greet(wrapped(row + i, n_row), col)
 
-    l_ints = [
-        load(source, target)
-        for source, target in (
-            (sends0_h, sends0), (sends1_h, sends1), (agg1_h, agg1),
-            (agg0_h, agg0), (cols0_h, cols0), (cols1_h, cols1),
-        )
-    ]
+    l_ints = [load(sends0_h, sends0), load(sends1_h, sends1), load(agg1_h, agg1)]
     l_rhs = load(rhs_h, rhs)
     l_diag0 = load(diag0_h, diag0)
     l_pro1 = load(pro1_h, pro1)
-    l_blocks0 = [load(blocks0_h.at[b], blocks0.at[b]) for b in range(nb)]
+    step = 2 if nb % 2 == 0 else 1
+    l_blocks0 = [
+        load(blocks0_h.at[pl.ds(b, step)], blocks0.at[pl.ds(b, step)]) for b in range(0, nb, step)
+    ]
 
     if not relayed:
         def greet_line(i, carry):
@@ -232,7 +233,7 @@
     def bulk_copy(d, g, there):
         return pltpu.make_async_remote_copy(
             src_ref=psend.at[d, g], dst_ref=precv.at[d, g],
-            send_sem=s_psend.at[d, g], recv_sem=s_precv.at[d, g],
+            send_sem=s_psend.at[d], recv_sem=s_precv.at[d],
             device_id=there, device_id_type=MESH,
         )
 
@@ -270,8 +271,42 @@
         lax.fori_loop(0, k, one, 0, unroll=7)
 
     def arrive(b):
-        l_blocks0[b].wait()
+        if b % step == 0:
+            l_blocks0[b // step].wait()
         split_blocks(b, blocks0, wide0, k0)
+
+    shares = s_csend.shape[0]
+    width = ncu // shares
+
+    def seat_copy(slot, share):
+        lanes = pl.ds(share * width, width)
+        return pltpu.make_async_remote_copy(
+            src_ref=cinv.at[:, lanes], dst_ref=cin.at[slot, :, lanes],
+            send_sem=s_csend.at[share], recv_sem=s_cin.at[share],
+            device_id=(my_tier * pair + pair - 1, my_seat), device_id_type=MESH,
+        )
+
+    def seat_start(share):
+        @pl.when(jnp.logical_not(solving))
+        def _():
+            seat_copy(my_slot, share).start()
+
+    def seat_ready(share):
+        if pair * reps > 1:
+            part = cin.at[pl.ds(0, pair * reps - 1), :, pl.ds(share * width, width)]
+            pltpu.make_async_copy(part, part, s_cin.at[share]).wait()
+
+        def one(c, carry):
+            at = pl.ds(pl.multiple_of(c * bs, bs), bs)
+            for m in range(pair):
+                piece = cin[m * reps : (m + 1) * reps, :, at].reshape(bs, bs)
+                h, t = two_terms(piece.T)
+                wide2[at, m * bs : (m + 1) * bs] = h
+                wide2[at, (pair + m) * bs : (pair + m + 1) * bs] = t
+            return carry
+
+        first = share * (ncb // shares)
+        lax.fori_loop(first, first + ncb // shares, one, 0, unroll=4 if ncb // shares % 4 == 0 else 1)
 
     l_rhs.wait()
     l_diag0.wait()
@@ -295,15 +330,27 @@
     start(level0, 0)
     l_pro1.wait()
     bulk_start(0)
-    l_cinv = load(cinv_h, cinv)
-    l_pro0 = load(pro0_h, pro0)
-    l_diag1 = load(diag1_h, diag1)
-    l_blocks1 = load(blocks1_h, blocks1)
+    l_late = [
+        load(source, target)
+        for source, target in (
+            (cols0_h, cols0), (agg0_h, agg0), (cols1_h, cols1), (cinv_h, cinv), (pro0_h, pro0),
+            (diag1_h, diag1),
+        )
+    ]
     own_ext(x0, ext0, nb)
     for b in range(nb1):
         aggf[b : b + 1, :] = jnp.full((1, bs), agg1[b].astype(F32))
-    for b in range(nb):
+    arrive(0)
+    l_blocks1 = load(blocks1_h, blocks1)
+    mixed = 3
+    for b in range(1, nb - mixed):
         arrive(b)
+    for copy in l_late[:3]:
+        copy.wait()
+    if mixed:
+        for b in range(nb - mixed, nb):
+            if b % step == 0:
+                l_blocks0[b // step].wait()
 
     def tell_far(jump):
         if relayed:
@@ -333,46 +380,21 @@
         part = dst.at[pl.ds(0, count)]
         pltpu.make_async_copy(part, part, sem).wait()
 
-    shares = s_csend.shape[0]
-    width = ncu // shares
-
-    def seat_copy(slot, share):
-        lanes = pl.ds(share * width, width)
-        return pltpu.make_async_remote_copy(
-            src_ref=cinv.at[:, lanes], dst_ref=cin.at[slot, :, lanes],
-            send_sem=s_csend.at[share], recv_sem=s_cin.at[share],
-            device_id=(my_tier * pair + pair - 1, my_seat), device_id_type=MESH,
-        )
-
-    def seat_start(share):
-        @pl.when(jnp.logical_not(solving))
-        def _():
-            seat_copy(my_slot, share).start()
-
-    def seat_ready(share):
-        if pair * reps > 1:
-            part = cin.at[pl.ds(0, pair * reps - 1), :, pl.ds(share * width, width)]
-            pltpu.make_async_copy(part, part, s_cin.at[share]).wait()
-
-        def one(c, carry):
-            at = pl.ds(pl.multiple_of(c * bs, bs), bs)
-            for m in range(pair):
-                piece = cin[m * reps : (m + 1) * reps, :, at].reshape(bs, bs)
-                h, t = two_terms(piece.T)
-                wide2[at, m * bs : (m + 1) * bs] = h
-                wide2[at, (pair + m) * bs : (pair + m + 1) * bs] = t
-            return carry
-
-        first = share * (ncb // shares)
-        lax.fori_loop(first, first + ncb // shares, one, 0, unroll=4 if ncb // shares % 4 == 0 else 1)
-
     def sweep0(e, into):
         finish(level0, e)
         if e == 0:
             tell_far(0)
         with jax.named_scope("sweep0"):
             ghost_ext(recv0, ext0, nb, e)
+            rest = []
+            if e == 0:
+                rest = [(b, i) for b in range(nb - mixed, nb) for i in range(k0)]
+            each = -(-len(rest) // max(nb - mixed, 1))
             for b in range(nb):
+                for late, i in rest[b * each : (b + 1) * each]:
+                    h, t = two_terms(blocks0[late, i].T)
+                    wide0[late, i * bs : (i + 1) * bs, :bs] = h
+                    wide0[late, i * bs : (i + 1) * bs, bs:] = t
                 c = coupled(b, cols0, ext0, wide0, k0)
                 v = x0[b]
                 into[b] = v + wfull0[b] * (rhs[b] - (dfull0[b] * v + c))
@@ -392,17 +414,9 @@
         start(level0, e0)
         own_ext(x0, ext0, nb)
 
-    for g in range(1, g1):
-        bulk_start(g)
     drain(2)
-    l_cinv.wait()
-
-    @pl.when(solving)
-    def _():
-        cin[my_slot] = cinv[...]
-        recva[me] = aggf[...]
-
-    l_pro0.wait()
+
+    l_late[4].wait()
     for b in range(nb):
         h, t = two_terms(pro0[b])
         down0[b * bs : (b + 1) * bs, :bs] = h
@@ -410,14 +424,22 @@
     l_blocks1.wait()
     for b in range(nb1):
         split_blocks(b, blocks1, wide1, k1)
-    l_diag1.wait()
+    l_late[5].wait()
     for b in range(nb1):
         d = jnp.broadcast_to(diag1[b : b + 1, :], (loads, bs))
         dfull1[b] = d
         wfull1[b] = OMEGA / d
 
+    hear_far(0)
+    l_late[3].wait()
+
+    @pl.when(solving)
+    def _():
+        cin[my_slot] = cinv[...]
+        recva[me] = aggf[...]
+
+    seat_start(0)
     finish(level0, e0)
-    hear_far(0)
     tell_far(1)
     with jax.named_scope("resid0"):
         ghost_ext(recv0, ext0, nb, e0)
@@ -438,7 +460,8 @@
     pack(x1, send1, sends1, 0, True)
     start(level1, 0)
     own_ext(x1, ext1, nb1)
-    seat_start(0)
+    for share in range(1, shares):
+        seat_start(share)
     drain(2)
     for b in range(nb1):
         h, t = two_terms(pro1[b])
@@ -475,12 +498,10 @@
         drain(2)
         own_ext(x1, ext1, nb1)
 
-    for share in range(1, shares):
-        seat_start(share)
-
     @pl.when(solving)
     def _():
-        seat_ready(0)
+        for share in range(shares):
+            seat_ready(share)
 
     base = [
         joined(stacked(b1[b] - dfull1[b] * x1[b]), down1[b], loads) for b in range(nb1)
@@ -494,6 +515,12 @@
             mine[b * loads : (b + 1) * loads, :] = base[b] - c
 
     to_solvers(mine, recvc, s_msend, 1)
+    for g in range(1, g1):
+        for d, (goes, there, _) in enumerate(directions):
+            @pl.when(goes)
+            def _():
+                bulk_copy(d, g - 1, there).wait_send()
+        bulk_start(g)
 
     @pl.when(solving)
     def _():
@@ -501,8 +528,6 @@
 
     @pl.when(solving)
     def _():
-        for share in range(1, shares):
-            seat_ready(share)
         with jax.named_scope("waitC1"):
             all_bytes(recva, n - 1, s_brecv.at[0])
             all_bytes(recvc, n - 1, s_brecv.at[1])
@@ -543,11 +568,11 @@
         recvx[my_place] = xs[...]
 
     for d, (_, _, comes) in enumerate(directions):
+        @pl.when(comes)
+        def _():
+            pltpu.make_async_copy(precv.at[d], precv.at[d], s_precv.at[d]).wait()
+
         for g in range(g1):
-            @pl.when(comes)
-            def _():
-                bulk_copy(d, g, (row, col)).wait_recv()
-
             h, t = two_terms(precv[d, g, :bs].T)
             up1[nb1 + d * g1 + g, :, :bs] = h
             up1[nb1 + d * g1 + g, :, bs:] = t
@@ -607,10 +632,9 @@
         drain(2)
         if i == NU - 1:
             for d, (goes, there, _) in enumerate(directions):
-                for g in range(g1):
-                    @pl.when(goes)
-                    def _():
-                        bulk_copy(d, g, there).wait_send()
+                @pl.when(goes)
+                def _():
+                    bulk_copy(d, g1 - 1, there).wait_send()
 
             @pl.when(jnp.logical_not(solving))
             def _():
@@ -654,7 +678,7 @@
     dma = pltpu.SemaphoreType.DMA
     scratch = [vm(a.shape, F32) for a in floats]
     scratch += [pltpu.SMEM(a.shape, jnp.int32) for a in ints]
-    scratch += [dma((nb + 3 + len(ints),))]
+    scratch += [dma((6 + (nb // 2 if nb % 2 == 0 else nb),))]
     scratch += [vm((nb, k0 * bs, 2 * bs), BF16)] + [vm((nb1, k1 * bs, 2 * bs), BF16)] * 2
     scratch += [vm((nb * bs, 2 * bs), BF16), vm((nb, bs, 2 * bs), BF16)]
     scratch += [vm((nb1, bs, 2 * bs), BF16), vm((nb1 + 4 * g1, bs, 2 * bs), BF16)]
@@ -671,7 +695,7 @@
     scratch += [vm((nb1 * loads, bs), F32), vm((n, nb1 * loads, bs), F32)]
     scratch += [vm((pair, loads, bs), F32), vm((ns, pair, loads, bs), F32)]
     scratch += [vm((n - 1, pair, loads, bs), F32)]
-    scratch += [dma((2, 4))] * 2 + [dma((4, g1))] * 2
+    scratch += [dma((2, 4))] * 2 + [dma((4,))] * 2
     scratch += [dma((shares,))] * 2 + [dma((1,))] * 3 + [dma((3,))]
     scratch += [pltpu.SemaphoreType.REGULAR((2,))]
     result = pl.pallas_call(

time: 42.1 us -> 41.4 us (0.983)
  Pallas kernels: 41.3 us -> 40.6 us
    pallas_call x1, Pallas kernels: 41.3 us -> 40.6 us  [on_device(): pl.pallas_call(functools.partial(kernel, n_row, n_col, pair), out_shape=p...]
where the time goes in v4:
time: 41.4 us; the launch traced here: 41.3 us
  Pallas kernels  40.6 us (98%)
  local copies, waits for them, and re-layouts  0.61 us (1%)
    pallas_call x1, Pallas kernels, on_device(): pl.pallas_call(functools.partial(kernel, n_row, n_col, pair), out_shape=p...  40.6 us

profile of v4, /device:TPU:0, one launch (start us, length us, event | category | flops | bytes accessed | tf_op | source)
XLA Modules:
  0.0 41.3 jit_solution(11466572445585886152)
XLA Ops:
  0.0 40.6 %shard_map.136 = f32[8,4,128]{2,1,0:T(4,128)S(1)} custom-call(s32[8,14]{1,0:T(8,128)} %bitcast.22, s32[4,4]{1,0:T(4,128)} %bitcast.24, s32[8]{0:T(128)} %bitcast.28, s32[2,14]{1,0:T(2,128)} %bitcast.25, s32[2,4]{1,0:T(2,128)} %bitcast.26, s32[2]{0:T(128)} %bitcast.29, f32[8,4,128]{2,1,0:T(4,128)} %bitcast.21, f32[8,128]{1,0:T(8,128)} %bitcast.23, ...), custom_call_target="tpu_custom_call" | custom-call | tf_op jit(solution)/shard_map/pallas_call | solution.py:701
  40.7 0.6 %copy.16 = f32[1,1,8,4,128]{4,3,2,1,0:T(4,128)} copy(f32[1,1,8,4,128]{4,3,2,1,0:T(4,128)S(1)} %bitcast.16) | data formatting | bytes 32768

commit v5 on v4

--- a/solution.py
+++ b/solution.py
@@ -90,9 +90,9 @@
     rhs, diag0, blocks0, pro0, diag1, blocks1, pro1, cinv,
     cols0, sends0, agg0, cols1, sends1, agg1,
     in_sem,
-    wide0, wide1, folded1, down0, up0, down1, up1, cin, wide2,
+    wide0, wide1, folded1, lifted1, down0, up0, down1, up1, cin, wide2,
     dfull0, wfull0, dfull1, wfull1,
-    ext0, ext1, x0, x1, b1, res0,
+    ext0, ext1, pext, x0, x1, b1, past1, res0,
     send0, recv0, send1, recv1, psend, precv,
     aggf, recva, mine, recvc, xs, recvx, tally,
     s_send, s_recv, s_psend, s_precv,
@@ -522,6 +522,9 @@
                 bulk_copy(d, g - 1, there).wait_send()
         bulk_start(g)
 
+    for b in range(nb1):
+        past1[b] = coupled(b, cols1, ext1, wide1, k1)
+
     @pl.when(solving)
     def _():
         recvc[me] = mine[...]
@@ -577,6 +580,18 @@
             up1[nb1 + d * g1 + g, :, :bs] = h
             up1[nb1 + d * g1 + g, :, bs:] = t
 
+    for b in range(nb1):
+        def carry_over(i, carry):
+            at = pl.ds(pl.multiple_of(i * bs, bs), bs)
+            block = wide1[b, at]
+            twice = jnp.concatenate([block, block], axis=0)
+            h, t = two_terms(folded(up1[cols1[b, i]], twice))
+            lifted1[b, at, :bs] = h
+            lifted1[b, at, bs:] = t
+            return carry
+
+        lax.fori_loop(0, k1, carry_over, 0, unroll=7)
+
     @pl.when(solving)
     def _():
         with jax.named_scope("waitC2"):
@@ -601,26 +616,23 @@
         return pieces
 
     pieces = lax.fori_loop(0, n_row // pair, pick, jnp.zeros(names.shape, F32), unroll=2)
-    for b in range(nb1):
-        x1[b] = x1[b] + joined(stacked(pieces[b]), up1[b], loads)
-    for d in range(4):
-        for g in range(g1):
-            v = nb1 + d * g1 + g
-            ghost = recv1[e1, d, g] + joined(stacked(pieces[v]), up1[v], loads)
-            ext1[v] = stacked(ghost)
+    for v in range(nb1 + 4 * g1):
+        pext[v] = stacked(pieces[v])
+    for b in range(nb1):
+        c = past1[b] + coupled(b, cols1, pext, lifted1, k1)
+        v = x1[b] + joined(pext[b], up1[b], loads)
+        x1[b] = v + wfull1[b] * (b1[b] - (dfull1[b] * v + c))
     e1 += 1
 
-    for i in range(NU):
+    for i in range(1, NU):
+        pack(x1, send1, sends1, e1, True)
+        start(level1, e1)
+        drain(2)
         own_ext(x1, ext1, nb1)
-        if i > 0:
-            finish(level1, e1)
-            ghost_ext(recv1, ext1, nb1, e1)
-            e1 += 1
+        finish(level1, e1)
+        ghost_ext(recv1, ext1, nb1, e1)
+        e1 += 1
         sweep1(b1, x1)
-        if i < NU - 1:
-            pack(x1, send1, sends1, e1, True)
-            start(level1, e1)
-            drain(2)
 
     own_ext(x1, ext1, nb1)
     for b in range(nb):
@@ -679,14 +691,15 @@
     scratch = [vm(a.shape, F32) for a in floats]
     scratch += [pltpu.SMEM(a.shape, jnp.int32) for a in ints]
     scratch += [dma((6 + (nb // 2 if nb % 2 == 0 else nb),))]
-    scratch += [vm((nb, k0 * bs, 2 * bs), BF16)] + [vm((nb1, k1 * bs, 2 * bs), BF16)] * 2
+    scratch += [vm((nb, k0 * bs, 2 * bs), BF16)] + [vm((nb1, k1 * bs, 2 * bs), BF16)] * 3
     scratch += [vm((nb * bs, 2 * bs), BF16), vm((nb, bs, 2 * bs), BF16)]
     scratch += [vm((nb1, bs, 2 * bs), BF16), vm((nb1 + 4 * g1, bs, 2 * bs), BF16)]
     scratch += [vm((pair * reps, owned, ncu), F32), vm((ncu, 2 * pair * bs), BF16)]
     scratch += [vm((nb, loads, bs), F32)] * 2
     scratch += [vm((nb1, loads, bs), F32)] * 2
     scratch += [vm((nb + 4 * g0, tall, bs), BF16), vm((nb1 + 4 * g1, tall, bs), BF16)]
-    scratch += [vm((nb, loads, bs), F32), vm((nb1, loads, bs), F32), vm((nb1, loads, bs), F32)]
+    scratch += [vm((nb1 + 4 * g1, tall, bs), BF16)]
+    scratch += [vm((nb, loads, bs), F32)] + [vm((nb1, loads, bs), F32)] * 3
     scratch += [vm((-(-2 * nb1 * loads // 16) * 16, nb * bs), BF16)]
     scratch += [vm((2 * NU, 4, g0, loads, bs), F32)] * 2
     scratch += [vm((2 * NU - 1, 4, g1, loads, bs), F32)] * 2

time: 41.4 us -> 41.3 us (level)
  no operation moved by 1% of the time
where the time goes in v5:
time: 41.3 us; the launch traced here: 41.1 us
  Pallas kernels  40.5 us (98%)
  local copies, waits for them, and re-layouts  0.61 us (1%)
    pallas_call x1, Pallas kernels, on_device(): pl.pallas_call(functools.partial(kernel, n_row, n_col, pair), out_shape=p...  40.5 us

profile of v5, /device:TPU:0, one launch (start us, length us, event | category | flops | bytes accessed | tf_op | source)
XLA Modules:
  0.0 41.1 jit_solution(3895244820072837447)
XLA Ops:
  0.0 40.5 %shard_map.136 = f32[8,4,128]{2,1,0:T(4,128)S(1)} custom-call(s32[8,14]{1,0:T(8,128)} %bitcast.22, s32[4,4]{1,0:T(4,128)} %bitcast.24, s32[8]{0:T(128)} %bitcast.28, s32[2,14]{1,0:T(2,128)} %bitcast.25, s32[2,4]{1,0:T(2,128)} %bitcast.26, s32[2]{0:T(128)} %bitcast.29, f32[8,4,128]{2,1,0:T(4,128)} %bitcast.21, f32[8,128]{1,0:T(8,128)} %bitcast.23, ...), custom_call_target="tpu_custom_call" | custom-call | tf_op jit(solution)/shard_map/pallas_call | solution.py:714
  40.5 0.6 %copy.16 = f32[1,1,8,4,128]{4,3,2,1,0:T(4,128)} copy(f32[1,1,8,4,128]{4,3,2,1,0:T(4,128)S(1)} %bitcast.16) | data formatting | bytes 32768

commit v6 on v5

--- a/solution.py
+++ b/solution.py
@@ -187,13 +187,24 @@
             precv[d] = jnp.zeros(precv.shape[1:], F32)
 
     order = []
+    partners = jnp.int32(0)
+    for goes, _, _ in directions:
+        partners = partners + jnp.where(goes, 1, 0)
+
+    def settle(part_of, sem):
+        for k in range(1, 5):
+            @pl.when(partners == k)
+            def _():
+                part = part_of(pl.ds(0, k))
+                pltpu.make_async_copy(part, part, sem).wait()
+
 
     def halo_copy(level, e, d, there):
         send, recv = level
         turn = order.index((level is level1, e)) % 2
         return pltpu.make_async_remote_copy(
             src_ref=send.at[e, d], dst_ref=recv.at[e, d],
-            send_sem=s_send.at[turn, d], recv_sem=s_recv.at[turn, d],
+            send_sem=s_send.at[turn], recv_sem=s_recv.at[turn],
             device_id=there, device_id_type=MESH,
         )
 
@@ -213,19 +224,15 @@
 
     def finish(level, e):
         with jax.named_scope("finish"):
-            for d, (_, there, comes) in enumerate(directions):
-                @pl.when(comes)
-                def _():
-                    halo_copy(level, e, d, (row, col)).wait_recv()
+            turn = order.index((level is level1, e)) % 2
+            settle(lambda some: level[1].at[e, some], s_recv.at[turn])
 
     def drain(back):
         if back > len(order):
             return
         upper, e = order[-back]
-        for d, (goes, there, _) in enumerate(directions):
-            @pl.when(goes)
-            def _():
-                halo_copy(level1 if upper else level0, e, d, there).wait_send()
+        recv = recv1 if upper else recv0
+        settle(lambda some: recv.at[e, some], s_send.at[(len(order) - back) % 2])
 
     level0 = (send0, recv0)
     level1 = (send1, recv1)
@@ -233,7 +240,7 @@
     def bulk_copy(d, g, there):
         return pltpu.make_async_remote_copy(
             src_ref=psend.at[d, g], dst_ref=precv.at[d, g],
-            send_sem=s_psend.at[d], recv_sem=s_precv.at[d],
+            send_sem=s_psend.at[0], recv_sem=s_precv.at[0],
             device_id=there, device_id_type=MESH,
         )
 
@@ -516,10 +523,7 @@
 
     to_solvers(mine, recvc, s_msend, 1)
     for g in range(1, g1):
-        for d, (goes, there, _) in enumerate(directions):
-            @pl.when(goes)
-            def _():
-                bulk_copy(d, g - 1, there).wait_send()
+        settle(lambda some: precv.at[some, 0], s_psend.at[0])
         bulk_start(g)
 
     for b in range(nb1):
@@ -570,11 +574,8 @@
             tell(wrapped(row + j, n_row), col)
         recvx[my_place] = xs[...]
 
-    for d, (_, _, comes) in enumerate(directions):
-        @pl.when(comes)
-        def _():
-            pltpu.make_async_copy(precv.at[d], precv.at[d], s_precv.at[d]).wait()
-
+    settle(lambda some: precv.at[some], s_precv.at[0])
+    for d in range(4):
         for g in range(g1):
             h, t = two_terms(precv[d, g, :bs].T)
             up1[nb1 + d * g1 + g, :, :bs] = h
@@ -643,10 +644,7 @@
         own_ext(x0, ext0, nb)
         drain(2)
         if i == NU - 1:
-            for d, (goes, there, _) in enumerate(directions):
-                @pl.when(goes)
-                def _():
-                    bulk_copy(d, g1 - 1, there).wait_send()
+            settle(lambda some: precv.at[some, 0], s_psend.at[0])
 
             @pl.when(jnp.logical_not(solving))
             def _():
@@ -708,7 +706,7 @@
     scratch += [vm((nb1 * loads, bs), F32), vm((n, nb1 * loads, bs), F32)]
     scratch += [vm((pair, loads, bs), F32), vm((ns, pair, loads, bs), F32)]
     scratch += [vm((n - 1, pair, loads, bs), F32)]
-    scratch += [dma((2, 4))] * 2 + [dma((4,))] * 2
+    scratch += [dma((2,))] * 2 + [dma((1,))] * 2
     scratch += [dma((shares,))] * 2 + [dma((1,))] * 3 + [dma((3,))]
     scratch += [pltpu.SemaphoreType.REGULAR((2,))]
     result = pl.pallas_call(

time: 41.3 us -> 41.1 us (level)
  no operation moved by 1% of the time
where the time goes in v6:
time: 41.1 us; the launch traced here: 41 us
  Pallas kernels  40.4 us (98%)
  local copies, waits for them, and re-layouts  0.61 us (1%)
    pallas_call x1, Pallas kernels, on_device(): pl.pallas_call(functools.partial(kernel, n_row, n_col, pair), out_shape=p...  40.4 us

profile of v6, /device:TPU:0, one launch (start us, length us, event | category | flops | bytes accessed | tf_op | source)
XLA Modules:
  0.0 41.0 jit_solution(13930994975834970562)
XLA Ops:
  0.0 40.4 %shard_map.136 = f32[8,4,128]{2,1,0:T(4,128)S(1)} custom-call(s32[8,14]{1,0:T(8,128)} %bitcast.22, s32[4,4]{1,0:T(4,128)} %bitcast.24, s32[8]{0:T(128)} %bitcast.28, s32[2,14]{1,0:T(2,128)} %bitcast.25, s32[2,4]{1,0:T(2,128)} %bitcast.26, s32[2]{0:T(128)} %bitcast.29, f32[8,4,128]{2,1,0:T(4,128)} %bitcast.21, f32[8,128]{1,0:T(8,128)} %bitcast.23, ...), custom_call_target="tpu_custom_call" | custom-call | tf_op jit(solution)/shard_map/pallas_call | solution.py:712
  40.4 0.6 %copy.16 = f32[1,1,8,4,128]{4,3,2,1,0:T(4,128)} copy(f32[1,1,8,4,128]{4,3,2,1,0:T(4,128)S(1)} %bitcast.16) | data formatting | bytes 32768
